TPU v7x, 128 devices: a whole 4x4x4 slice. The times are simulated.
128 devices in a mesh: gx: 8 (over y, core), gy: 16 (over x, z).
Axes of the slice: x: 4, y: 4, z: 4, core: 2. Of those that a mesh axis runs over, the one named last changes fastest.
Arguments:
- voxels_fine: bfloat16 [1024, 64, 512], P(('gx', 'gy')), may hold values from -6 to 6
- gain_fine: float32 [64], replicated, may hold values from 0.5 to 2
- gain_middle: float32 [128], replicated, may hold values from 0.5 to 2
- gain_coarse: float32 [256], replicated, may hold values from 0.5 to 2
- kernel_fine: bfloat16 [27, 64, 64], replicated, may hold values from -0.15625 to 0.15625
- kernel_middle: bfloat16 [27, 128, 128], replicated, may hold values from -0.109375 to 0.109375
- kernel_coarse: bfloat16 [27, 256, 256], replicated, may hold values from -0.078125 to 0.078125
- lift_middle: bfloat16 [128, 64], replicated, may hold values from -0.75 to 0.75
- lift_coarse: bfloat16 [256, 128], replicated, may hold values from -0.5 to 0.5
- links_fine: int32 [1024, 26], P(('gx', 'gy')), may hold values from 0 to 1072, as said below
- links_middle: int32 [256, 26], P(('gx', 'gy')), may hold values from 0 to 524, as said below
- links_coarse: int32 [128, 26], P(('gx', 'gy')), may hold values from 0 to 262, as said below
- sends_fine: int32 [128, 1024], P(('gx', 'gy')), may hold values from -1 to 47, as said below
- sends_middle: int32 [128, 512], P(('gx', 'gy')), may hold values from -1 to 11, as said below
- sends_coarse: int32 [128, 256], P(('gx', 'gy')), may hold values from -1 to 5, as said below
- parents_middle: int32 [256, 8], P(('gx', 'gy')), may hold values from 0 to 136
- parents_coarse: int32 [128, 8], P(('gx', 'gy')), may hold values from 0 to 130
- uplinks_middle: int32 [128, 128], P(('gx', 'gy')), may hold values from -1 to 7, as said below
- uplinks_coarse: int32 [128, 128], P(('gx', 'gy')), may hold values from -1 to 1, as said below
Outputs:
- output_fine: bfloat16 [1024, 64, 512], P(('gx', 'gy'))
- output_middle: bfloat16 [256, 128, 512], P(('gx', 'gy'))
- output_coarse: bfloat16 [128, 256, 512], P(('gx', 'gy'))
Inputs may be any that keep to these rules, and one draw needn't show every extreme that they name: `links_fine`: rows 48 and up name received slabs or the zero row of the step. `links_middle`: rows 12 and up name received slabs or the zero row of the step. `links_coarse`: rows 6 and up name received slabs or the zero row of the step. `sends_fine`: -1 marks an empty slot. `sends_middle`: -1 marks an empty slot. `sends_coarse`: -1 marks an empty slot. `uplinks_middle`: -1 marks an empty slot. `uplinks_coarse`: -1 marks an empty slot.
All inputs are finite; a program needn't handle non-finite values.
Results may differ from a plain program's by a relative error of at most 0.015.
Values may be sent and summed in bfloat16 or wider, within the bound.
A program may use at most 192 MiB of HBM per device.

v0:
```python
import jax
import jax.numpy as jnp
from jax import lax
from jax.sharding import PartitionSpec as P

EPSILON = 1e-06
DIRECTIONS = [
    (along_x, along_y, along_z)
    for along_x in (-1, 0, 1)
    for along_y in (-1, 0, 1)
    for along_z in (-1, 0, 1)
    if (along_x, along_y, along_z) != (0, 0, 0)
]


def cut_along(array, dim, peers):
    before, after = (array.shape[:dim], array.shape[dim + 1 :])
    return jnp.moveaxis(array.reshape(*before, peers, -1, *after), dim, 0)


def joined_along(blocks, dim):
    shape = list(blocks.shape[1:])
    shape[dim] *= blocks.shape[0]
    return jnp.moveaxis(blocks, 0, dim).reshape(shape)


def one_exchange(array, axis, axes, splits, concats):
    sizes = [lax.axis_size(a) for a in axes]
    blocks = cut_along(array, splits[0], sizes[0])
    blocks = jnp.moveaxis(cut_along(blocks, splits[1] + 1, sizes[1]), 0, 1)
    inside = blocks.shape[2:]
    blocks = blocks.reshape(-1, *inside)
    blocks = lax.all_to_all(blocks, axis, split_axis=0, concat_axis=0, tiled=True)
    blocks = joined_along(blocks.reshape(*sizes, *inside), concats[0] + 1)
    return joined_along(blocks, concats[1])


def leading_axis(direction):
    for position in range(3):
        if direction[position] != 0:
            return position
    return 0


def activate(hidden, scales):
    values = hidden.astype(jnp.float32)
    mean_sq = jnp.mean(values * values, axis=1, keepdims=True)
    scaled = values * lax.rsqrt(mean_sq + EPSILON) * scales[None, :, None]
    return jax.nn.silu(scaled).astype(jnp.bfloat16)


def brick_faces(active):
    bricks, channels = (active.shape[0], active.shape[1])
    volume = active.reshape(bricks, channels, 8, 8, 8)
    layers = [
        volume[:, :, 7],
        volume[:, :, 0],
        volume[:, :, :, 7],
        volume[:, :, :, 0],
        volume[:, :, :, :, 7],
        volume[:, :, :, :, 0],
    ]
    return jnp.stack(layers, axis=1).reshape(bricks * 6, channels * 64)


def assemble(active, slabs):
    bricks, channels = (active.shape[0], active.shape[1])
    pieces = {(0, 0, 0): active.reshape(bricks, channels, 8, 8, 8)}
    for placing, direction in enumerate(DIRECTIONS):
        slab_cut = slabs[:, placing].reshape(bricks, channels, 8, 8)
        leading = leading_axis(direction)
        others = [position for position in range(3) if position != leading]
        chosen = tuple(
            (
                slice(None) if direction[position] == 0 else 7 if direction[position] < 0 else 0
                for position in others
            )
        )
        selected = slab_cut[(slice(None), slice(None)) + chosen]
        shape = (bricks, channels) + tuple((8 if step == 0 else 1 for step in direction))
        pieces[direction] = selected.reshape(shape)
    planes = []
    for along_x in (-1, 0, 1):
        lines = []
        for along_y in (-1, 0, 1):
            lines.append(
                jnp.concatenate(
                    [pieces[along_x, along_y, along_z] for along_z in (-1, 0, 1)], axis=4
                )
            )
        planes.append(jnp.concatenate(lines, axis=3))
    return jnp.concatenate(planes, axis=2).reshape(bricks, channels, 1000)


def interior(full):
    bricks, outputs = (full.shape[0], full.shape[1])
    widened = jnp.pad(full, ((0, 0), (0, 0), (0, 22)))
    lattice = widened.reshape(bricks, outputs, 8, 100)[:, :, :, :80].reshape(
        bricks, outputs, 8, 8, 10
    )[:, :, :, :, :8]
    return lattice.reshape(bricks, outputs, 512)


def convolve(padded, kernel):
    bricks, channels = (padded.shape[0], padded.shape[1])
    outputs = kernel.shape[1]
    total = jnp.zeros((bricks, outputs, 778), jnp.float32)
    for along_x in range(3):
        for along_y in range(3):
            base = along_x * 100 + along_y * 10
            first = 9 * along_x + 3 * along_y
            stacked = jnp.concatenate(
                [padded[:, :, base + shift : base + shift + 778] for shift in range(3)], axis=1
            )
            block = kernel[first : first + 3].transpose(1, 0, 2).reshape(outputs, 3 * channels)
            total = total + jnp.einsum(
                "ok,bkv->bov", block, stacked, preferred_element_type=jnp.float32
            )
    return interior(total)


def pool_blocks(output):
    bricks, channels = (output.shape[0], output.shape[1])
    values = output.astype(jnp.float32).reshape(bricks, channels, 4, 2, 4, 2, 4, 2)
    return jnp.mean(values, axis=(3, 5, 7)).astype(jnp.bfloat16).reshape(bricks, channels * 64)


def place_octants(gathered):
    parents = gathered.shape[0]
    channels = gathered.shape[2] // 64
    volume = gathered.reshape(parents, 2, 2, 2, channels, 4, 4, 4)
    return volume.transpose(0, 4, 1, 5, 2, 6, 3, 7).reshape(parents, channels, 512)


def outgoing_rows(table, senders):
    picked = senders[0]
    taken = jnp.take(table, jnp.maximum(picked, 0), axis=0)
    return jnp.where((picked >= 0)[:, None], taken, jnp.zeros((), table.dtype))


def route_slabs(outgoing):
    across = lax.axis_size("gx")
    along = lax.axis_size("gy")
    slot_count = outgoing.shape[0] // (across * along)
    arranged = outgoing.reshape(across, along, slot_count, outgoing.shape[1])
    moved = one_exchange(arranged, ("gx", "gy"), ("gx", "gy"), (0, 1), (0, 1))
    return moved.reshape(outgoing.shape)


def route_pooled(outgoing):
    across = lax.axis_size("gx")
    along = lax.axis_size("gy")
    slot_count = outgoing.shape[0] // (across * along)
    arranged = outgoing.reshape(across, along, slot_count, outgoing.shape[1])
    moved = one_exchange(arranged, ("gx", "gy"), ("gx", "gy"), (0, 1), (0, 1))
    return moved.reshape(outgoing.shape)


def halo_level(hidden, scales, kernel, links, senders):
    bricks, channels = (hidden.shape[0], hidden.shape[1])
    active = activate(hidden, scales)
    faces = brick_faces(active)
    arrived = route_slabs(outgoing_rows(faces, senders))
    blanks = jnp.zeros((1, faces.shape[1]), jnp.bfloat16)
    source = jnp.concatenate([faces, arrived, blanks], axis=0)
    slabs = jnp.take(source, links.reshape(-1), axis=0).reshape(bricks, 26, channels * 64)
    padded = assemble(active, slabs)
    return (hidden.astype(jnp.float32) + convolve(padded, kernel)).astype(jnp.bfloat16)


def pool_level(output, lift, links, senders):
    parents = links.shape[0]
    blocks = pool_blocks(output)
    arrived = route_pooled(outgoing_rows(blocks, senders))
    blanks = jnp.zeros((1, blocks.shape[1]), jnp.bfloat16)
    source = jnp.concatenate([blocks, arrived, blanks], axis=0)
    gathered = jnp.take(source, links.reshape(-1), axis=0).reshape(parents, 8, blocks.shape[1])
    parent_grid = place_octants(gathered)
    return jnp.einsum("oc,bcv->bov", lift, parent_grid, preferred_element_type=jnp.float32).astype(
        jnp.bfloat16
    )


def per_device(
    voxels_fine,
    gain_fine,
    gain_middle,
    gain_coarse,
    kernel_fine,
    kernel_middle,
    kernel_coarse,
    lift_middle,
    lift_coarse,
    links_fine,
    links_middle,
    links_coarse,
    sends_fine,
    sends_middle,
    sends_coarse,
    parents_middle,
    parents_coarse,
    uplinks_middle,
    uplinks_coarse,
):
    output_fine = halo_level(voxels_fine, gain_fine, kernel_fine, links_fine, sends_fine)
    hidden_middle = pool_level(output_fine, lift_middle, parents_middle, uplinks_middle)
    output_middle = halo_level(
        hidden_middle, gain_middle, kernel_middle, links_middle, sends_middle
    )
    hidden_coarse = pool_level(output_middle, lift_coarse, parents_coarse, uplinks_coarse)
    output_coarse = halo_level(
        hidden_coarse, gain_coarse, kernel_coarse, links_coarse, sends_coarse
    )
    return (output_fine, output_middle, output_coarse)


def solution(mesh):
    placed = (
        P(("gx", "gy"), None, None),
        P(),
        P(),
        P(),
        P(),
        P(),
        P(),
        P(),
        P(),
        P(("gx", "gy"), None),
        P(("gx", "gy"), None),
        P(("gx", "gy"), None),
        P(("gx", "gy"), None),
        P(("gx", "gy"), None),
        P(("gx", "gy"), None),
        P(("gx", "gy"), None),
        P(("gx", "gy"), None),
        P(("gx", "gy"), None),
        P(("gx", "gy"), None),
    )
    return jax.shard_map(
        per_device,
        mesh=mesh,
        in_specs=placed,
        out_specs=(
            P(("gx", "gy"), None, None),
            P(("gx", "gy"), None, None),
            P(("gx", "gy"), None, None),
        ),
        check_vma=False,
    )
```

profile of v0, /device:TPU:1, one launch (start us, length us, event | category | flops | bytes accessed | tf_op | source)
XLA Modules:
  0.0 1118.4 jit_solution(1231821342556836640)
XLA Ops:
  9.4 9.9 reshape.856
  19.5 7.8 gather_fusion
  27.4 7.4 fusion
  34.8 12.4 %all-to-all-start = ((bf16[128,1,1,8,4096]{4,3,2,1,0:T(8,128)(2,1)}), bf16[128,1,1,8,4096]{4,3,2,1,0:T(8,128)(2,1)}, u32[]{:S(2)}, u32[]{:S(2)}) async-start(bf16[128,1,1,8,4096]{4,3,2,1,0:T(8,128)(2,1)} %fusion), calls=%async_computation | async-start | bytes 16777216 | tf_op jit(solution)/shard_map/all_to_all | solution.py:33
  55.1 92.3 %all-to-all-done = bf16[128,1,1,8,4096]{4,3,2,1,0:T(8,128)(2,1)} async-done(((bf16[128,1,1,8,4096]{4,3,2,1,0:T(8,128)(2,1)}), bf16[128,1,1,8,4096]{4,3,2,1,0:T(8,128)(2,1)}, u32[]{:S(2)}, u32[]{:S(2)}) %all-to-all-start) | async-done | bytes 8388640 | tf_op jit(solution)/shard_map/all_to_all | solution.py:33
  147.4 7.4 pad_maximum_fusion
  154.8 9.1 gather_fusion.1
  320.2 10.6 fusion.204
  457.9 8.6 all-to-all-start.1
  467.0 18.1 %all-to-all-done.1 = bf16[128,2,2048]{2,1,0:T(2,128)(2,1)S(1)} async-done(((bf16[128,2,2048]{2,1,0:T(2,128)(2,1)}), bf16[128,2,2048]{2,1,0:T(2,128)(2,1)S(1)}, u32[]{:S(2)}, u32[]{:S(2)}) %all-to-all-start.1) | async-done | bytes 1048608 | tf_op jit(solution)/shard_map/all_to_all | solution.py:33
  488.2 10.3 gather.67
  504.5 6.5 copy.1112
  519.5 7.8 gather_fusion.4
  527.3 13.1 %gather.69 = bf16[128,1,1,4,8192]{4,3,0,2,1:T(4,128)(2,1)} reshape(bf16[512,8192]{1,0:T(8,128)(2,1)} %gather_fusion.4) | data formatting | bytes 16777216 | tf_op jit(solution)/shard_map/jit(_take)/gather | solution.py:137
  540.4 8.5 fusion.1
  560.5 95.2 %all-to-all-done.2 = bf16[128,1,1,4,8192]{4,3,2,1,0:T(4,128)(2,1)} async-done(((bf16[128,1,1,4,8192]{4,3,2,1,0:T(4,128)(2,1)}), bf16[128,1,1,4,8192]{4,3,2,1,0:T(4,128)(2,1)}, u32[]{:S(2)}, u32[]{:S(2)}) %all-to-all-start.2) | async-done | bytes 8388640 | tf_op jit(solution)/shard_map/all_to_all | solution.py:33
  655.7 12.5 %reshape_reshape.19 = bf16[512,8192]{1,0:T(8,128)(2,1)} reshape(bf16[8,16,1,4,8192]{4,3,1,0,2:T(4,128)(2,1)} %bitcast.86) | data formatting | bytes 16777216 | tf_op jit(solution)/shard_map/reshape;reshape | solution.py:147
  668.3 8.5 pad_maximum_fusion.1
  676.8 6.4 gather_fusion.5
  736.1 6.7 fusion.210
  767.6 8.8 all-to-all-start.3
  778.0 27.8 %all-to-all-done.3 = bf16[128,2,4096]{2,1,0:T(2,128)(2,1)S(1)} async-done(((bf16[128,2,4096]{2,1,0:T(2,128)(2,1)}), bf16[128,2,4096]{2,1,0:T(2,128)(2,1)S(1)}, u32[]{:S(2)}, u32[]{:S(2)}) %all-to-all-start.3) | async-done | bytes 2097184 | tf_op jit(solution)/shard_map/all_to_all | solution.py:33
  805.9 6.8 reshape.1166
  818.3 10.9 gather.75
  835.3 6.5 copy.1206
  848.2 9.0 gather_fusion.8
  857.3 14.1 %gather.77 = bf16[128,1,1,2,16384]{4,3,0,2,1:T(2,128)(2,1)} reshape(bf16[256,16384]{1,0:T(8,128)(2,1)} %gather_fusion.8) | data formatting | bytes 16777216 | tf_op jit(solution)/shard_map/jit(_take)/gather | solution.py:137
  871.4 11.6 %broadcast_select_fusion.1 = bf16[128,1,1,2,16384]{4,3,2,1,0:T(2,128)(2,1)} fusion(pred[128,2]{1,0:T(8,128)(4,1)S(1)} %ge.142, pred[128,2]{1,0:T(8,128)(4,1)S(1)} %le.141, bf16[128,1,1,2,16384]{4,3,0,2,1:T(2,128)(2,1)} %gather.77), kind=kLoop, calls=%fused_computation.11 | loop fusion | flops 8388608 | bytes 16777728 | tf_op jit(solution)/shard_map/jit(_where)/select_n | solution.py:138
  907.5 82.0 %all-to-all-done.4 = bf16[128,1,1,2,16384]{4,3,2,1,0:T(2,128)(2,1)} async-done(((bf16[128,1,1,2,16384]{4,3,2,1,0:T(2,128)(2,1)}), bf16[128,1,1,2,16384]{4,3,2,1,0:T(2,128)(2,1)}, u32[]{:S(2)}, u32[]{:S(2)}) %all-to-all-start.4) | async-done | bytes 8388640 | tf_op jit(solution)/shard_map/all_to_all | solution.py:33
  989.5 13.1 %reshape_reshape.21 = bf16[256,16384]{1,0:T(8,128)(2,1)} reshape(bf16[8,16,1,2,16384]{4,3,1,0,2:T(2,128)(2,1)} %bitcast.154) | data formatting | bytes 16777216 | tf_op jit(solution)/shard_map/reshape;reshape | solution.py:147
  1002.6 47.3 %concatenate.263 = bf16[263,16384]{1,0:T(8,128)(2,1)} concatenate(bf16[1,16384]{1,0:T(2,128)(2,1)S(1)} %stack.23, bf16[1,16384]{1,0:T(2,128)(2,1)S(1)} %stack.24, bf16[1,16384]{1,0:T(2,128)(2,1)S(1)} %stack.25, bf16[1,16384]{1,0:T(2,128)(2,1)S(1)} %stack.26, bf16[1,16384]{1,0:T(2,128)(2,1)S(1)} %stack.27, bf16[1,16384]{1,0:T(2,128)(2,1)S(1)} %stack.28, ...), dimensions={0} | concatenate | bytes 17235968 | tf_op jit(solution)/shard_map/concatenate | solution.py:165
  1049.9 6.4 gather_fusion.9
  (693 shorter events, 510.9 us)
Async XLA Ops:
  0.6 841.2 %copy-start = (bf16[256,128]{1,0:T(8,128)(2,1)S(1)}, bf16[256,128]{1,0:T(8,128)(2,1)}, u32[]{:S(2)}) copy-start(bf16[256,128]{1,0:T(8,128)(2,1)} %param.27) | copy-start | bytes 196612
  34.8 12.5 %copy-start.32 = (bf16[27,64,64]{2,1,0:T(8,128)(2,1)S(1)}, bf16[27,64,64]{2,1,0:T(8,128)(2,1)}, u32[]{:S(2)}) copy-start(bf16[27,64,64]{2,1,0:T(8,128)(2,1)} %param.23) | copy-start | bytes 663556
  34.8 13.2 %copy-start.73 = (s32[8,26]{1,0:T(8,128)S(1)}, s32[8,26]{1,0:T(8,128)}, u32[]{:S(2)}) copy-start(s32[8,26]{1,0:T(8,128)} %param.28) | copy-start | bytes 2500
  34.8 19.0 %copy-start.78 = (s32[2,8]{1,0:T(2,128)S(1)}, s32[2,8]{1,0:T(2,128)}, u32[]{:S(2)}) copy-start(s32[2,8]{1,0:T(2,128)} %param.34) | copy-start | bytes 196
  34.8 19.1 %copy-start.89 = (s32[1,128]{1,0:T(1,128)S(1)}, s32[1,128]{1,0:T(1,128)}, u32[]{:S(2)}) copy-start(s32[1,128]{1,0:T(1,128)} %param.36) | copy-start | bytes 1540
  34.8 112.6 %all-to-all-start = ((bf16[128,1,1,8,4096]{4,3,2,1,0:T(8,128)(2,1)}), bf16[128,1,1,8,4096]{4,3,2,1,0:T(8,128)(2,1)}, u32[]{:S(2)}, u32[]{:S(2)}) async-start(bf16[128,1,1,8,4096]{4,3,2,1,0:T(8,128)(2,1)} %fusion), calls=%async_computation | async-start | bytes 16777216 | tf_op jit(solution)/shard_map/all_to_all | solution.py:33
  260.4 10.4 copy-start.48
  264.9 16.6 %copy-start.47 = (bf16[8,4096]{1,0:T(8,128)(2,1)S(1)}, bf16[8,4096]{1,0:T(8,128)(2,1)}, u32[]{:S(2)}) copy-start(bf16[8,4096]{1,0:T(8,128)(2,1)} %get-tuple-element.43) | copy-start | bytes 196612
  272.9 13.5 %copy-start.46 = (bf16[8,4096]{1,0:T(8,128)(2,1)S(1)}, bf16[8,4096]{1,0:T(8,128)(2,1)}, u32[]{:S(2)}) copy-start(bf16[8,4096]{1,0:T(8,128)(2,1)} %get-tuple-element.44) | copy-start | bytes 196612
  278.1 12.2 %copy-start.45 = (bf16[8,4096]{1,0:T(8,128)(2,1)S(1)}, bf16[8,4096]{1,0:T(8,128)(2,1)}, u32[]{:S(2)}) copy-start(bf16[8,4096]{1,0:T(8,128)(2,1)} %get-tuple-element.45) | copy-start | bytes 196612
  290.3 7.8 copy-start.44
  292.9 10.5 copy-start.43
  456.3 10.2 copy-start.79
  456.3 10.3 copy-start.88
  456.3 10.4 copy-start.75
  457.9 27.2 %all-to-all-start.1 = ((bf16[128,2,2048]{2,1,0:T(2,128)(2,1)}), bf16[128,2,2048]{2,1,0:T(2,128)(2,1)S(1)}, u32[]{:S(2)}, u32[]{:S(2)}) async-start(bf16[128,2,2048]{2,1,0:T(2,128)(2,1)} %reshape.1163), calls=%async_computation.1 | async-start | bytes 2097152 | tf_op jit(solution)/shard_map/all_to_all | solution.py:33
  504.5 6.5 copy-start.72
  504.5 6.9 copy-start.85
  548.9 106.8 %all-to-all-start.2 = ((bf16[128,1,1,4,8192]{4,3,2,1,0:T(4,128)(2,1)}), bf16[128,1,1,4,8192]{4,3,2,1,0:T(4,128)(2,1)}, u32[]{:S(2)}, u32[]{:S(2)}) async-start(bf16[128,1,1,4,8192]{4,3,2,1,0:T(4,128)(2,1)} %fusion.1), calls=%async_computation.2 | async-start | bytes 16777216 | tf_op jit(solution)/shard_map/all_to_all | solution.py:33
  767.6 10.0 copy-start.76
  767.6 10.4 copy-start.92
  767.6 38.3 %all-to-all-start.3 = ((bf16[128,2,4096]{2,1,0:T(2,128)(2,1)}), bf16[128,2,4096]{2,1,0:T(2,128)(2,1)S(1)}, u32[]{:S(2)}, u32[]{:S(2)}) async-start(bf16[128,2,4096]{2,1,0:T(2,128)(2,1)} %reshape.1165), calls=%async_computation.3 | async-start | bytes 4194304 | tf_op jit(solution)/shard_map/all_to_all | solution.py:33
  835.3 6.9 copy-start.77
  883.0 106.5 %all-to-all-start.4 = ((bf16[128,1,1,2,16384]{4,3,2,1,0:T(2,128)(2,1)}), bf16[128,1,1,2,16384]{4,3,2,1,0:T(2,128)(2,1)}, u32[]{:S(2)}, u32[]{:S(2)}) async-start(bf16[128,1,1,2,16384]{4,3,2,1,0:T(2,128)(2,1)} %broadcast_select_fusion.1), calls=%async_computation.4 | async-start | bytes 16777216 | tf_op jit(solution)/shard_map/all_to_all | solution.py:33
  895.9 9.6 copy-start.2
  1089.7 7.4 copy-start.55
  1090.2 8.2 copy-start.54
  1091.2 7.9 copy-start.53
  1100.6 6.3 copy-start.80
  1100.6 6.3 copy-start.81
  1100.6 6.3 copy-start.82
  1100.7 6.3 copy-start.83
  (66 other events, 128.5 us)
where the time goes:
time: 1130 us; the launch traced here: 1120 us
  local copies, waits for them, and re-layouts  655 us (58%)
  waiting for transfers between devices  316 us (28%)
  other arithmetic  83.2 us (7%)
  starting transfers between devices  41.8 us (4%)
  matrix products  19.4 us (2%)
    all_to_all x5, waiting for transfers between devices, one_exchange(): lax.all_to_all(blocks, axis, split_axis=0, concat_axis=0, tiled=True)  316 us
    unnamed x286, local copies, waits for them, and re-layouts  150 us
    slice x84, local copies, waits for them, and re-layouts, assemble(): selected = slab_cut[(slice(None), slice(None)) + chosen]  91.1 us
    another operation x60, local copies, waits for them, and re-layouts, assemble(): slab_cut = slabs[:, placing].reshape(bricks, channels, 8, 8)  70.2 us
    gather x7, local copies, waits for them, and re-layouts, outgoing_rows(): taken = jnp.take(table, jnp.maximum(picked, 0), axis=0)  56.5 us
    another operation x74, local copies, waits for them, and re-layouts, assemble(): pieces[direction] = selected.reshape(shape)  52 us
    concatenate x1, local copies, waits for them, and re-layouts, halo_level(): source = jnp.concatenate([faces, arrived, blanks], axis=0)  47.3 us
    all_to_all x5, starting transfers between devices, one_exchange(): lax.all_to_all(blocks, axis, split_axis=0, concat_axis=0, tiled=True)  41.8 us
  transfers between devices with their start and end apart: 5, of which 5 were waited for; matrix products, arithmetic and copies ran while one was open for 3% of the time, Pallas kernels for 0%

commit v1 on v0

v1 whole, which is shorter than its diff:
```python
import functools

import jax
import jax.numpy as jnp
import numpy as np
from jax import lax
from jax.experimental import pallas as pl
from jax.experimental.pallas import tpu as pltpu
from jax.sharding import PartitionSpec as P

EPSILON = 1e-06
MESH = pl.DeviceIdType.MESH
BF16, F32, I32 = jnp.bfloat16, jnp.float32, jnp.int32
RING = 4
CORES = 2
VMEM_LIMIT = 60 * 1024 * 1024
DIRECTIONS = [
    (a, b, c) for a in (-1, 0, 1) for b in (-1, 0, 1) for c in (-1, 0, 1) if (a, b, c) != (0, 0, 0)
]


def face_sources():
    ids = np.arange(512).reshape(8, 8, 8)
    layers = [ids[7], ids[0], ids[:, 7], ids[:, 0], ids[:, :, 7], ids[:, :, 0]]
    return np.stack(layers).reshape(1, 384).astype(np.int32)


def halo_cells():
    return [
        (x, y, z)
        for x in range(10)
        for y in range(10)
        for z in range(10)
        if not all(1 <= v <= 8 for v in (x, y, z))
    ]


def halo_sources():
    out = np.full((1, 512), -1, np.int32)
    for n, cell in enumerate(halo_cells()):
        t = tuple(-1 if v == 0 else 1 if v == 9 else 0 for v in cell)
        lead = next(p for p in range(3) if t[p] != 0)
        u, v = [7 if t[p] < 0 else 0 if t[p] > 0 else cell[p] - 1 for p in range(3) if p != lead]
        out[0, n] = DIRECTIONS.index(t) * 64 + u * 8 + v
    return out


def padded_sources():
    out = np.full((1, 1280), -1, np.int32)
    halo = {cell: n for n, cell in enumerate(halo_cells())}
    for x in range(10):
        for y in range(10):
            for z in range(10):
                if (x, y, z) in halo:
                    source = 512 + halo[x, y, z]
                else:
                    source = (x - 1) * 64 + (y - 1) * 8 + z - 1
                out[0, x * 128 + y * 10 + z] = source
    return out


def shift_sources():
    out = np.zeros((9, 2, 8, 8), np.int32)
    for d in range(9):
        for q in range(2):
            for y in range(8):
                for z in range(8):
                    out[d, q, y, z] = q * 128 + (y + d // 3) * 10 + z + d % 3
    return out.reshape(1, 1152)


def octant_sources():
    out = np.zeros((8, 8, 8), np.int32)
    for x in range(8):
        for y in range(8):
            for z in range(8):
                octant = 4 * (x // 4) + 2 * (y // 4) + z // 4
                out[x, y, z] = octant * 64 + (x % 4) * 16 + (y % 4) * 4 + z % 4
    return out.reshape(1, 512)


def selection(depth, sources):
    rows = lax.broadcasted_iota(I32, (depth, sources.shape[1]), 0)
    return jnp.where(rows == sources, 1.0, 0.0).astype(BF16)


def mm(a, b):
    return jnp.dot(a, b, preferred_element_type=F32)


def activate(values, gain):
    mean_sq = jnp.mean(values * values, axis=0, keepdims=True)
    scaled = values * lax.rsqrt(mean_sq + EPSILON) * gain
    return (scaled / (1.0 + jnp.exp(-scaled))).astype(BF16)


def write_faces(bricks, channels, active_ref, sources_ref, table_ref):
    faces = mm(active_ref[...], selection(512, sources_ref[...])).astype(BF16)
    for b in range(bricks):
        for pair in range(3):
            table_ref[3 * b + pair] = faces[
                b * channels : (b + 1) * channels, pair * 128 : (pair + 1) * 128
            ]


def enter_fine(bricks, channels, hidden_ref, gain_ref, sources_ref, active_ref, table_ref):
    for b in range(bricks):
        rows = slice(b * channels, (b + 1) * channels)
        active_ref[rows] = activate(hidden_ref[rows].astype(F32), gain_ref[...])
    write_faces(bricks, channels, active_ref, sources_ref, table_ref)


def enter_coarser(
    bricks, below, channels, parts_ref, lift_ref, gain_ref, sources_ref, hidden_ref, active_ref, table_ref
):
    for b in range(bricks):
        own = slice(b * below, (b + 1) * below)
        rows = slice(b * channels, (b + 1) * channels)
        grid = sum(parts_ref[x, own].astype(F32) for x in range(RING)).astype(BF16)
        hidden = mm(lift_ref[...], grid).astype(BF16)
        hidden_ref[rows] = hidden
        active_ref[rows] = activate(hidden.astype(F32), gain_ref[...])
    write_faces(bricks, channels, active_ref, sources_ref, table_ref)


def pack(
    bricks, channels, tiles, ways, index_ref, table_hbm, sources_ref, out_ref, table_ref, gathered_ref, choose_ref, sem
):
    dest = pl.program_id(0)

    @pl.when(dest == 0)
    def _():
        copy = pltpu.make_async_copy(table_hbm, table_ref.at[pl.ds(0, tiles)], sem)
        copy.start()
        table_ref[tiles] = jnp.zeros((channels, 128), BF16)
        choose_ref[...] = selection(ways * 64, sources_ref[...])
        copy.wait()

    lanes = lax.broadcasted_iota(I32, (channels, 128), 1)
    low = lanes < 64

    def brick(b, carry):
        rows = pl.ds(pl.multiple_of(b * channels, channels), channels)
        for way in range(0, ways, 2):
            base = (dest * bricks + b) * ways + way
            first, second = index_ref[base], index_ref[base + 1]
            one = table_ref[first // 2]
            two = table_ref[second // 2]
            one_turned = jnp.concatenate([one[:, 64:], one[:, :64]], axis=1)
            two_turned = jnp.concatenate([two[:, 64:], two[:, :64]], axis=1)
            one = jnp.where(first % 2 == 0, one, one_turned)
            two = jnp.where(second % 2 == 0, two_turned, two)
            gathered_ref[rows, way * 64 : way * 64 + 128] = jnp.where(low, one, two)
        return carry

    lax.fori_loop(0, bricks, brick, 0)
    out_ref[0] = mm(gathered_ref[...], choose_ref[...]).astype(BF16)


def leave(
    bricks,
    channels,
    pooled,
    active_ref,
    parts_ref,
    hidden_ref,
    kernel_ref,
    place_ref,
    shift_ref,
    out_ref,
    *rest,
):
    if pooled:
        table_ref, rest = rest[0], rest[1:]
    source_ref, padded_ref, shifts_ref, weight_ref, moved_ref = rest
    source_ref[:, 0:512] = active_ref[...]
    source_ref[:, 512:1024] = sum(parts_ref[x].astype(F32) for x in range(RING)).astype(BF16)
    padded_ref[...] = mm(source_ref[...], selection(1024, place_ref[...])).astype(BF16)
    shifts_ref[...] = selection(256, shift_ref[...])
    for dx in range(3):
        for d in range(9):
            weight_ref[
                dx * channels : (dx + 1) * channels, d * channels : (d + 1) * channels
            ] = kernel_ref[dx * 9 + d]

    def brick(b, carry):
        start = b * channels if isinstance(b, int) else pl.multiple_of(b * channels, channels)
        rows = pl.ds(start, channels)
        planes = jnp.concatenate(
            [padded_ref[rows, pair * 256 : (pair + 1) * 256] for pair in range(5)], axis=0
        )
        moved = mm(planes, shifts_ref[...]).astype(BF16)
        for pair in range(5):
            for d in range(9):
                moved_ref[d * channels : (d + 1) * channels, pair * 128 : (pair + 1) * 128] = moved[
                    pair * channels : (pair + 1) * channels, d * 128 : (d + 1) * 128
                ]
        total = hidden_ref[rows].astype(F32)
        for dx in range(3):
            part = mm(weight_ref[dx * channels : (dx + 1) * channels], moved_ref[...])
            total = total + part[:, dx * 64 : dx * 64 + 512]
        out_ref[rows] = total.astype(BF16)
        return carry

    if bricks > 1:
        lax.fori_loop(0, bricks, brick, 0)
    else:
        brick(0, 0)
    if pooled:
        voxel = lax.broadcasted_iota(I32, (512, 64), 0)
        block = (
            lax.shift_left(lax.shift_right_logical(voxel, 7), 4)
            + lax.shift_left(lax.shift_right_logical(voxel, 4) & 3, 2)
            + (lax.shift_right_logical(voxel, 1) & 3)
        )
        column = lax.broadcasted_iota(I32, (512, 64), 1)
        average = jnp.where(block == column, 0.125, 0.0).astype(BF16)
        blocks = mm(out_ref[...], average).astype(BF16)
        for b in range(bricks):
            table_ref[b // 2, :, (b % 2) * 64 : (b % 2) * 64 + 64] = blocks[
                b * channels : (b + 1) * channels
            ]


def shape(*dims, dtype=BF16):
    return jax.ShapeDtypeStruct(dims, dtype)


def whole(count):
    return [pl.BlockSpec(memory_space=pltpu.VMEM)] * count


PARAMS = pltpu.CompilerParams(vmem_limit_bytes=VMEM_LIMIT)


def place_self():
    across, along = lax.axis_index("gx"), lax.axis_index("gy")
    return across // CORES, across % CORES, along // RING, along % RING


def gather_kernel(rows, channels, own_ref, all_ref, stage_ref, send_sems, recv_sems, local_sems):
    y, core, x, z = place_self()
    half, quarter = channels // 2, channels // 4

    def peer(dy, dz, other=False):
        new_core = 1 - core if other else core
        return (((y + dy) % RING) * CORES + new_core, x * RING + (z + dz) % RING)

    def slot(dy, dz, other=False):
        new_core = 1 - core if other else core
        return (((y + dy) % RING) * CORES + new_core) * RING + (z + dz) % RING

    barrier = pltpu.get_barrier_semaphore()
    neighbours = [peer(1, 0), peer(3, 0), peer(0, 1), peer(0, 3), peer(0, 0, True)]
    for device in neighbours:
        pl.semaphore_signal(barrier, inc=1, device_id=device, device_id_type=MESH)

    come = pltpu.make_async_copy(own_ref, stage_ref, local_sems.at[0])
    come.start()
    pl.semaphore_wait(barrier, len(neighbours))

    started = []
    counter = [0]

    def send(dy, dz, start, size, device):
        n = counter[0]
        counter[0] += 1
        part = pl.ds(start, size)
        source = own_ref.at[:, part] if (dy, dz) == (0, 0) else all_ref.at[slot(dy, dz), :, part]
        copy = pltpu.make_async_remote_copy(
            src_ref=source,
            dst_ref=all_ref.at[slot(dy, dz), :, part],
            send_sem=send_sems.at[n],
            recv_sem=recv_sems.at[n],
            device_id=device,
            device_id_type=MESH,
        )
        copy.start()
        started.append(copy)
        return n

    def arrived(n, dy, dz, start, size, other=False):
        view = all_ref.at[slot(dy, dz, other), :, pl.ds(start, size)]
        pltpu.make_async_remote_copy(
            src_ref=view,
            dst_ref=view,
            send_sem=send_sems.at[n],
            recv_sem=recv_sems.at[n],
            device_id=neighbours[0],
            device_id_type=MESH,
        ).wait_recv()

    def sibling(dy, dz, start, size):
        n = send(dy, dz, start, size, neighbours[4])
        siblings.append((n, dy, dz, start, size))

    siblings = []
    UP, DOWN = 1, 3

    def off(axis, k):
        return (k % RING, 0) if axis == "y" else (0, k % RING)

    def both(axis, dy, dz, start, size):
        events = []
        for step in (UP, DOWN):
            sy, sz = off(axis, step)
            n = send(dy, dz, start, size, peer(sy, sz))
            events.append((n, axis, step, (dy - sy) % RING, (dz - sz) % RING, start, size))
        return events

    def relay(event):
        n, axis, step, dy, dz, start, size = event
        piece = size // 2
        begin = start if step == UP else start + piece
        sy, sz = off(axis, step)
        m = send(dy, dz, begin, piece, peer(sy, sz))
        return (m, axis, step, (dy - sy) % RING, (dz - sz) % RING, begin, piece)

    def wait(event):
        n, axis, step, dy, dz, start, size = event
        arrived(n, dy, dz, start, size)

    parts = [("z", "y", 0), ("y", "z", half)]
    first, second = [], []
    for axis, other_axis, start in parts:
        first.append(both(axis, 0, 0, start, half))
    for axis, other_axis, start in parts:
        second += both(other_axis, 0, 0, start, half)
    sibling(0, 0, 0, channels)
    come.wait()
    go = pltpu.make_async_copy(stage_ref, all_ref.at[slot(0, 0)], local_sems.at[1])
    go.start()

    relays = []
    for (axis, other_axis, start), events in zip(parts, first):
        passed = []
        for event in events:
            wait(event)
            passed.append(relay(event))
            _, _, _, dy, dz, _, _ = event
            second += both(other_axis, dy, dz, start, half)
            sibling(dy, dz, start, half)
        relays.append(passed)
    for (axis, other_axis, start), passed in zip(parts, relays):
        for event in passed:
            wait(event)
        _, _, _, dy, dz, _, _ = passed[0]
        second += both(other_axis, dy, dz, start, half)
        sibling(dy, dz, start, half)
    last = []
    for event in second:
        wait(event)
        _, _, _, dy, dz, start, size = event
        last.append(relay(event))
        sibling(dy, dz, start, size)
    for event in last:
        wait(event)
        _, _, _, dy, dz, start, size = event
        sibling(dy, dz, start, size)
    for n, dy, dz, start, size in siblings:
        arrived(n, dy, dz, start, size, True)
    for copy in started:
        copy.wait_send()
    go.wait()


COPIES = 92


def gather_plane(table, number):
    rows, channels = table.shape[0], table.shape[1]
    members = RING * RING * CORES
    return pl.pallas_call(
        functools.partial(gather_kernel, rows, channels),
        out_shape=shape(members, rows, channels, 128),
        in_specs=[pl.BlockSpec(memory_space=pl.ANY)],
        out_specs=pl.BlockSpec(memory_space=pl.ANY),
        scratch_shapes=[
            pltpu.VMEM((rows, channels, 128), BF16),
            pltpu.SemaphoreType.DMA((COPIES,)),
            pltpu.SemaphoreType.DMA((COPIES,)),
            pltpu.SemaphoreType.DMA((2,)),
        ],
        compiler_params=pltpu.CompilerParams(collective_id=number, has_side_effects=True),
        name=f"gather_{number}",
    )(table)


def swap_along_x(parts):
    groups = [[x * RING + z for x in range(RING)] for z in range(RING)]
    return lax.all_to_all(
        parts, "gy", split_axis=0, concat_axis=0, tiled=True, axis_index_groups=groups
    )


def send_halves(table, index, ways, sources, bricks, number):
    channels = table.shape[1]
    gathered = gather_plane(table, number)
    tiles = gathered.shape[0] * gathered.shape[1]
    gathered = gathered.reshape(tiles, channels, 128)
    parts = pl.pallas_call(
        functools.partial(pack, bricks, channels, tiles, ways),
        out_shape=shape(RING, bricks * channels, 512),
        grid_spec=pltpu.PrefetchScalarGridSpec(
            num_scalar_prefetch=1,
            grid=(RING,),
            in_specs=[
                pl.BlockSpec(memory_space=pl.ANY),
                pl.BlockSpec((1, 512), lambda i, index: (0, 0)),
            ],
            out_specs=pl.BlockSpec((1, bricks * channels, 512), lambda i, index: (i, 0, 0)),
            scratch_shapes=[
                pltpu.VMEM((tiles + 1, channels, 128), BF16),
                pltpu.VMEM((bricks * channels, ways * 64), BF16),
                pltpu.VMEM((ways * 64, 512), BF16),
                pltpu.SemaphoreType.DMA,
            ],
        ),
        compiler_params=PARAMS,
        name=f"pack_{number}",
    )(index, gathered, sources)
    return swap_along_x(parts)


def convolve(active, parts, hidden, kernel, bricks, pooled):
    channels = kernel.shape[1]
    outs = [shape(bricks * channels, 512)]
    if pooled:
        outs.append(shape(bricks // 2, channels, 128))
    return pl.pallas_call(
        functools.partial(leave, bricks, channels, pooled),
        out_shape=outs,
        in_specs=whole(6),
        out_specs=whole(len(outs)),
        scratch_shapes=[
            pltpu.VMEM((bricks * channels, 1024), BF16),
            pltpu.VMEM((bricks * channels, 1280), BF16),
            pltpu.VMEM((256, 1152), BF16),
            pltpu.VMEM((3 * channels, 9 * channels), BF16),
            pltpu.VMEM((9 * channels, 640), BF16),
        ],
        compiler_params=PARAMS,
        name=f"convolve_{channels}",
    )(active, parts, hidden, kernel, jnp.asarray(padded_sources()), jnp.asarray(shift_sources()))


def look_up(table, positions):
    hit = positions[:, None] == jnp.arange(table.shape[0], dtype=I32)[None, :]
    return jnp.sum(jnp.where(hit, table[None, :], 0), axis=1)


def owned_rows(links, received, width):
    members, slots = received.shape
    rows = links.reshape(-1)
    me = lax.axis_index("gx") * lax.axis_size("gy") + lax.axis_index("gy")
    remote = rows - width
    is_remote = (remote >= 0) & (remote < members * slots)
    picked = look_up(received.reshape(-1), remote)
    away = jnp.where(is_remote & (picked >= 0), (remote // slots) * width + picked, -1)
    return jnp.where(rows < width, me * width + rows, away)


def rows_here(asked, width):
    x = lax.axis_index("gy") // RING
    owner, row = asked // width, asked % width
    across, along = owner // (RING * RING), owner % (RING * RING)
    here = (asked >= 0) & (along // RING == x)
    members = RING * RING * CORES
    found = (across * RING + along % RING) * width + row
    return jnp.where(here, found, members * width).reshape(-1).astype(I32)


def per_device(
    voxels_fine,
    gain_fine,
    gain_middle,
    gain_coarse,
    kernel_fine,
    kernel_middle,
    kernel_coarse,
    lift_middle,
    lift_coarse,
    links_fine,
    links_middle,
    links_coarse,
    sends_fine,
    sends_middle,
    sends_coarse,
    parents_middle,
    parents_coarse,
    uplinks_middle,
    uplinks_coarse,
):
    members = lax.axis_size("gx") * lax.axis_size("gy")
    bricks = [voxels_fine.shape[0], links_middle.shape[0], links_coarse.shape[0]]
    width = [6 * bricks[0], 6 * bricks[1], 6 * bricks[2], bricks[0], bricks[1]]
    links = [links_fine, links_middle, links_coarse, parents_middle, parents_coarse]
    sends = [
        s.reshape(members, -1)
        for s in (sends_fine, sends_middle, sends_coarse, uplinks_middle, uplinks_coarse)
    ]
    slots = [s.shape[1] for s in sends]
    received = lax.all_to_all(
        jnp.concatenate(sends, axis=1), ("gx", "gy"), split_axis=0, concat_axis=0, tiled=True
    )
    wanted, begin = [], 0
    for n in range(5):
        wanted.append(owned_rows(links[n], received[:, begin : begin + slots[n]], width[n]))
        begin += slots[n]
    counts = [w.shape[0] for w in wanted]
    joined = jnp.concatenate(wanted)
    asked = swap_along_x(jnp.broadcast_to(joined[None], (RING, joined.shape[0])))
    index, begin = [], 0
    for n in range(5):
        index.append(rows_here(asked[:, begin : begin + counts[n]], width[n]))
        begin += counts[n]

    faces, halos, octants = (
        jnp.asarray(face_sources()),
        jnp.asarray(halo_sources()),
        jnp.asarray(octant_sources()),
    )
    channels = [kernel_fine.shape[1], kernel_middle.shape[1], kernel_coarse.shape[1]]
    gains = [g.reshape(-1, 1) for g in (gain_fine, gain_middle, gain_coarse)]

    hidden = voxels_fine.reshape(bricks[0] * channels[0], 512)
    active, table = pl.pallas_call(
        functools.partial(enter_fine, bricks[0], channels[0]),
        out_shape=[shape(bricks[0] * channels[0], 512), shape(3 * bricks[0], channels[0], 128)],
        in_specs=whole(3),
        out_specs=whole(2),
        compiler_params=PARAMS,
        name="enter_0",
    )(hidden, gains[0], faces)
    kernels, lifts = (kernel_fine, kernel_middle, kernel_coarse), (None, lift_middle, lift_coarse)
    outputs = []
    for level in range(3):
        if level:
            parts = send_halves(pooled_table, index[2 + level], 8, octants, bricks[level], 2 * level)
            size = bricks[level] * channels[level]
            hidden, active, table = pl.pallas_call(
                functools.partial(enter_coarser, bricks[level], channels[level - 1], channels[level]),
                out_shape=[
                    shape(size, 512),
                    shape(size, 512),
                    shape(3 * bricks[level], channels[level], 128),
                ],
                in_specs=whole(4),
                out_specs=whole(3),
                compiler_params=PARAMS,
                name=f"enter_{level}",
            )(parts, lifts[level], gains[level], faces)
        parts = send_halves(table, index[level], 26, halos, bricks[level], 2 * level + 1)
        results = convolve(active, parts, hidden, kernels[level], bricks[level], level < 2)
        outputs.append(results[0].reshape(bricks[level], channels[level], 512))
        pooled_table = results[1] if level < 2 else None
    return tuple(outputs)


def solution(mesh):
    split = ("gx", "gy")
    placed = (P(split, None, None),) + (P(),) * 8 + (P(split, None),) * 10
    return jax.shard_map(
        per_device,
        mesh=mesh,
        in_specs=placed,
        out_specs=(P(split, None, None),) * 3,
        check_vma=False,
    )
```

time: 1130 us -> 355 us (0.31)
  local copies, waits for them, and re-layouts: 655 us -> 16 us
  waiting for transfers between devices: 316 us -> 58.2 us
  Pallas kernels: 0 us -> 217 us
  other arithmetic: 83.2 us -> 12.3 us
  matrix products: 19.4 us -> 0 us
  blocking collectives: 0 us -> 19.2 us
  starting transfers between devices: 41.8 us -> 30 us
    all_to_all x5 -> x6, waiting for transfers between devices: 316 us -> 58.2 us  [the longest x5 54.9 us: swap_along_x(): lax.all_to_all(parts, 'gy', split_axis=0, concat_axis=0, tiled=True, axis...]
    pallas_call x0 -> x16, Pallas kernels: none -> 217 us  [the longest x5 136 us: gather_plane(): pl.pallas_call(functools.partial(gather_kernel, rows, channels), out_shap...]
    another operation x149 -> x0, local copies, waits for them, and re-layouts: 158 us -> none  [the longest x60 70.2 us: assemble(): slab_cut = slabs[:, placing].reshape(bricks, channels, 8, 8)]
    unnamed x286 -> x17, local copies, waits for them, and re-layouts: 150 us -> 5.16 us
    slice x113 -> x3, local copies, waits for them, and re-layouts: 144 us -> 0.35 us  [per_device(): received[:, begin:begin + slots[n]]]
    gather x16 -> x0, local copies, waits for them, and re-layouts: 104 us -> none  [the longest x7 56.5 us: outgoing_rows(): taken = jnp.take(table, jnp.maximum(picked, 0), axis=0)]
    concatenate x12 -> x2, local copies, waits for them, and re-layouts: 53.1 us -> 0.84 us  [the longest x1 0.76 us: per_device(): jnp.concatenate(sends, axis=1)]
    select_n x15 -> x10, other arithmetic: 36 us -> 1.82 us  [the longest x5 1.38 us: owned_rows(): return jnp.where(rows < width, me * width + rows, away)]
  transfers between devices with their start and end apart: 5 -> 6, of which waited for: 5 -> 5; matrix products, arithmetic and copies ran while one was open for 3% -> 4% of each run, Pallas kernels for 0% -> 12%
where the time goes in v1:
time: 355 us; the launch traced here: 354 us
  Pallas kernels  217 us (61%)
  waiting for transfers between devices  58.2 us (16%)
  starting transfers between devices  30 us (8%)
  blocking collectives  19.2 us (5%)
  local copies, waits for them, and re-layouts  16 us (5%)
  other arithmetic  12.3 us (3%)
    pallas_call x5, Pallas kernels, gather_plane(): pl.pallas_call(functools.partial(gather_kernel, rows, channels), out_shap...  136 us
    all_to_all x5, waiting for transfers between devices, swap_along_x(): lax.all_to_all(parts, 'gy', split_axis=0, concat_axis=0, tiled=True, axis...  54.9 us
    pallas_call x5, Pallas kernels, send_halves(): pl.pallas_call(functools.partial(pack, bricks, channels, tiles, ways), ou...  48.6 us
    pallas_call x3, Pallas kernels, convolve(): pl.pallas_call(functools.partial(leave, bricks, channels, pooled), out_sh...  25.5 us
    all_to_all x1, blocking collectives, swap_along_x(): lax.all_to_all(parts, 'gy', split_axis=0, concat_axis=0, tiled=True, axis...  19.2 us
    all_to_all x5, starting transfers between devices, swap_along_x(): lax.all_to_all(parts, 'gy', split_axis=0, concat_axis=0, tiled=True, axis...  18.5 us
    all_to_all x1, starting transfers between devices, per_device(): lax.all_to_all(jnp.concatenate(sends, axis=1), ('gx', 'gy'), split_axis=0...  11.5 us
  transfers between devices with their start and end apart: 6, of which 5 were waited for; matrix products, arithmetic and copies ran while one was open for 4% of the time, Pallas kernels for 12%

profile of v1, /device:TPU:1, one launch (start us, length us, event | category | flops | bytes accessed | tf_op | source)
XLA Modules:
  0.0 353.6 jit_solution(1632528502266712823)
XLA Ops:
  1.1 1.3 reduce.13
  2.6 1.3 reduce.14
  7.8 11.5 %all-to-all-start = ((s32[128,1,16]{2,1,0:T(1,128)}), s32[128,1,16]{2,1,0:T(1,128)S(1)}, u32[]{:S(2)}, u32[]{:S(2)}) async-start(s32[128,1,16]{2,1,0:T(1,128)} %bitcast.5), calls=%async_computation | async-start | bytes 131072 | tf_op jit(solution)/shard_map/all_to_all | solution.py:503
  25.5 3.3 all-to-all-done
  32.6 3.2 all-to-all-start.1
  35.8 1.4 copy.57.gain_ref
  37.2 2.6 enter_0.1
  39.8 41.0 %gather_1.1 = bf16[32,24,64,128]{3,2,1,0:T(8,128)(2,1)} custom-call(bf16[24,64,128]{2,1,0:T(8,128)(2,1)} %get-tuple-element.16.own_ref), custom_call_target="tpu_custom_call" | custom-call | tf_op jit(solution)/shard_map/gather_1/pallas_call | solution.py:373
  81.6 19.5 %pack_1.1 = bf16[4,512,512]{2,1,0:T(8,128)(2,1)} custom-call(s32[832]{0:T(1024)} %reshape.152.index_ref, bf16[768,64,128]{2,1,0:T(8,128)(2,1)} %bitcast.38, s32[1,512]{1,0:T(1,128)} %constant.374.clone.sources_ref), custom_call_target="tpu_custom_call" | custom-call | tf_op jit(solution)/shard_map/pack_1/pallas_call | solution.py:401
  101.0 4.6 %all-to-all-start.2 = ((bf16[4,512,512]{2,1,0:T(8,128)(2,1)}), bf16[4,512,512]{2,1,0:T(8,128)(2,1)S(1)}, u32[]{:S(2)}, u32[]{:S(2)}) async-start(bf16[4,512,512]{2,1,0:T(8,128)(2,1)} %pack_1.1), calls=%async_computation.2 | async-start | bytes 4194304 | tf_op jit(solution)/shard_map/all_to_all | solution.py:391
  106.3 25.4 %all-to-all-done.2.parts_ref = bf16[4,512,512]{2,1,0:T(8,128)(2,1)S(1)} async-done(((bf16[4,512,512]{2,1,0:T(8,128)(2,1)}), bf16[4,512,512]{2,1,0:T(8,128)(2,1)S(1)}, u32[]{:S(2)}, u32[]{:S(2)}) %all-to-all-start.2) | async-done | bytes 2097184 | tf_op jit(solution)/shard_map/all_to_all | solution.py:391
  131.7 1.3 copy-done
  133.1 11.5 %convolve_64.1 = (bf16[512,512]{1,0:T(8,128)(2,1)}, bf16[4,64,128]{2,1,0:T(8,128)(2,1)}) custom-call(bf16[512,512]{1,0:T(8,128)(2,1)} %get-tuple-element.15.active_ref, bf16[4,512,512]{2,1,0:T(8,128)(2,1)} %copy-done, bf16[512,512]{1,0:T(8,128)(2,1)} %bitcast.48, bf16[27,64,64]{2,1,0:T(8,128)(2,1)} %kernel_ref.3, s32[1,1280]{1,0:T(1,128)} %constant.376.clone.place_ref, ...), custom_call_target="tpu_custom_call" | custom-call | tf_op jit(solution)/shard_map/convolve_64/pallas_call | solution.py:430
  144.6 20.7 %gather_2.1 = bf16[32,4,64,128]{3,2,1,0:T(8,128)(2,1)} custom-call(bf16[4,64,128]{2,1,0:T(8,128)(2,1)} %get-tuple-element.18.own_ref), custom_call_target="tpu_custom_call" | custom-call | tf_op jit(solution)/shard_map/gather_2/pallas_call | solution.py:373
  165.4 5.7 %pack_2.1 = bf16[4,128,512]{2,1,0:T(8,128)(2,1)} custom-call(s32[64]{0:T(128)} %reshape.155.index_ref, bf16[128,64,128]{2,1,0:T(8,128)(2,1)} %bitcast.41, s32[1,512]{1,0:T(1,128)} %constant.375.clone.sources_ref), custom_call_target="tpu_custom_call" | custom-call | tf_op jit(solution)/shard_map/pack_2/pallas_call | solution.py:401
  171.1 3.7 %all-to-all-start.3 = ((bf16[4,128,512]{2,1,0:T(8,128)(2,1)}), bf16[4,128,512]{2,1,0:T(8,128)(2,1)S(1)}, u32[]{:S(2)}, u32[]{:S(2)}) async-start(bf16[4,128,512]{2,1,0:T(8,128)(2,1)} %pack_2.1), calls=%async_computation.3 | async-start | bytes 1048576 | tf_op jit(solution)/shard_map/all_to_all | solution.py:391
  177.0 7.1 %all-to-all-done.3.parts_ref = bf16[4,128,512]{2,1,0:T(8,128)(2,1)S(1)} async-done(((bf16[4,128,512]{2,1,0:T(8,128)(2,1)}), bf16[4,128,512]{2,1,0:T(8,128)(2,1)S(1)}, u32[]{:S(2)}, u32[]{:S(2)}) %all-to-all-start.3) | async-done | bytes 524320 | tf_op jit(solution)/shard_map/all_to_all | solution.py:391
  184.9 2.3 enter_1.1
  187.2 26.8 %gather_3.1 = bf16[32,6,128,128]{3,2,1,0:T(8,128)(2,1)} custom-call(bf16[6,128,128]{2,1,0:T(8,128)(2,1)} %get-tuple-element.20.own_ref), custom_call_target="tpu_custom_call" | custom-call | tf_op jit(solution)/shard_map/gather_3/pallas_call | solution.py:373
  214.0 10.0 %pack_3.1 = bf16[4,256,512]{2,1,0:T(8,128)(2,1)} custom-call(s32[208]{0:T(256)} %reshape.158.index_ref, bf16[192,128,128]{2,1,0:T(8,128)(2,1)} %bitcast.40, s32[1,512]{1,0:T(1,128)} %constant.374.clone.sources_ref), custom_call_target="tpu_custom_call" | custom-call | tf_op jit(solution)/shard_map/pack_3/pallas_call | solution.py:401
  224.1 3.5 all-to-all-start.4
  228.3 14.4 %all-to-all-done.4.parts_ref = bf16[4,256,512]{2,1,0:T(8,128)(2,1)S(1)} async-done(((bf16[4,256,512]{2,1,0:T(8,128)(2,1)}), bf16[4,256,512]{2,1,0:T(8,128)(2,1)S(1)}, u32[]{:S(2)}, u32[]{:S(2)}) %all-to-all-start.4) | async-done | bytes 1048608 | tf_op jit(solution)/shard_map/all_to_all | solution.py:391
  243.7 6.5 %convolve_128.1 = (bf16[256,512]{1,0:T(8,128)(2,1)}, bf16[1,128,128]{2,1,0:T(8,128)(2,1)}) custom-call(bf16[256,512]{1,0:T(8,128)(2,1)} %get-tuple-element.19.active_ref, bf16[4,256,512]{2,1,0:T(8,128)(2,1)} %copy-done.1, bf16[256,512]{1,0:T(8,128)(2,1)} %get-tuple-element.21.hidden_ref, bf16[27,128,128]{2,1,0:T(8,128)(2,1)} %kernel_ref.4, ...), custom_call_target="tpu_custom_call" | custom-call | tf_op jit(solution)/shard_map/convolve_128/pallas_call | solution.py:430
  250.2 20.3 %gather_4.1 = bf16[32,1,128,128]{3,2,1,0:T(8,128)(2,1)} custom-call(bf16[1,128,128]{2,1,0:T(8,128)(2,1)} %get-tuple-element.23.own_ref), custom_call_target="tpu_custom_call" | custom-call | tf_op jit(solution)/shard_map/gather_4/pallas_call | solution.py:373
  270.5 4.9 %pack_4.1 = bf16[4,128,512]{2,1,0:T(8,128)(2,1)} custom-call(s32[32]{0:T(128)} %reshape.161.index_ref, bf16[32,128,128]{2,1,0:T(8,128)(2,1)} %bitcast.42, s32[1,512]{1,0:T(1,128)} %constant.375.clone.sources_ref), custom_call_target="tpu_custom_call" | custom-call | tf_op jit(solution)/shard_map/pack_4/pallas_call | solution.py:401
  275.4 3.5 all-to-all-start.5
  280.4 7.9 %all-to-all-done.5.parts_ref = bf16[4,128,512]{2,1,0:T(8,128)(2,1)S(1)} async-done(((bf16[4,128,512]{2,1,0:T(8,128)(2,1)}), bf16[4,128,512]{2,1,0:T(8,128)(2,1)S(1)}, u32[]{:S(2)}, u32[]{:S(2)}) %all-to-all-start.5) | async-done | bytes 524320 | tf_op jit(solution)/shard_map/all_to_all | solution.py:391
  289.1 2.5 enter_2.1
  291.6 26.8 %gather_5.1 = bf16[32,3,256,128]{3,2,1,0:T(8,128)(2,1)} custom-call(bf16[3,256,128]{2,1,0:T(8,128)(2,1)} %get-tuple-element.25.own_ref), custom_call_target="tpu_custom_call" | custom-call | tf_op jit(solution)/shard_map/gather_5/pallas_call | solution.py:373
  318.4 8.5 %pack_5.1 = bf16[4,256,512]{2,1,0:T(8,128)(2,1)} custom-call(s32[104]{0:T(128)} %reshape.164.index_ref, bf16[96,256,128]{2,1,0:T(8,128)(2,1)} %bitcast.39, s32[1,512]{1,0:T(1,128)} %constant.374.clone.sources_ref), custom_call_target="tpu_custom_call" | custom-call | tf_op jit(solution)/shard_map/pack_5/pallas_call | solution.py:401
  326.9 19.2 %all_to_all.46.parts_ref = bf16[4,256,512]{2,1,0:T(8,128)(2,1)} all-to-all(bf16[4,256,512]{2,1,0:T(8,128)(2,1)} %pack_5.1), channel_id=1, replica_groups={{0,4,8,12},{1,5,9,13},{2,6,10,14},{3,7,11,15},{16,20,24,28},{17,21,25,2..., dimensions={0} | all-to-all | bytes 2097152 | tf_op jit(solution)/shard_map/all_to_all | solution.py:391
  346.1 7.5 %convolve_256.1 = bf16[256,512]{1,0:T(8,128)(2,1)} custom-call(bf16[256,512]{1,0:T(8,128)(2,1)} %get-tuple-element.24.active_ref, bf16[4,256,512]{2,1,0:T(8,128)(2,1)} %all_to_all.46.parts_ref, bf16[256,512]{1,0:T(8,128)(2,1)} %get-tuple-element.26.hidden_ref, bf16[27,256,256]{2,1,0:T(8,128)(2,1)} %kernel_ref.5, s32[1,1280]{1,0:T(1,128)} %constant.376.clone.place_ref, ...), custom_call_target="tpu_custom_call" | custom-call | tf_op jit(solution)/shard_map/convolve_256/pallas_call | solution.py:430
  (71 shorter events, 22.8 us)
Async XLA Ops:
  7.8 21.0 %all-to-all-start = ((s32[128,1,16]{2,1,0:T(1,128)}), s32[128,1,16]{2,1,0:T(1,128)S(1)}, u32[]{:S(2)}, u32[]{:S(2)}) async-start(s32[128,1,16]{2,1,0:T(1,128)} %bitcast.5), calls=%async_computation | async-start | bytes 131072 | tf_op jit(solution)/shard_map/all_to_all | solution.py:503
  32.6 48.3 %all-to-all-start.1 = ((s32[4,1,310]{2,1,0:T(1,128)}), s32[4,1,310]{2,1,0:T(1,128)S(1)}, u32[]{:S(2)}, u32[]{:S(2)}) async-start(s32[4,1,310]{2,1,0:T(1,128)} %broadcast_in_dim.131), calls=%async_computation.1 | async-start | bytes 12288 | tf_op jit(solution)/shard_map/all_to_all | solution.py:391
  101.0 30.7 %all-to-all-start.2 = ((bf16[4,512,512]{2,1,0:T(8,128)(2,1)}), bf16[4,512,512]{2,1,0:T(8,128)(2,1)S(1)}, u32[]{:S(2)}, u32[]{:S(2)}) async-start(bf16[4,512,512]{2,1,0:T(8,128)(2,1)} %pack_1.1), calls=%async_computation.2 | async-start | bytes 4194304 | tf_op jit(solution)/shard_map/all_to_all | solution.py:391
  131.7 1.4 copy-start
  144.6 30.1 %copy-start.4 = (bf16[128,64]{0,1:T(8,128)(2,1)S(1)}, bf16[128,64]{0,1:T(8,128)(2,1)}, u32[]{:S(2)}) copy-start(bf16[128,64]{0,1:T(8,128)(2,1)} %param.35) | copy-start | bytes 49156
  144.6 30.8 %copy-start.6 = (f32[128]{0:T(128)S(1)}, f32[128]{0:T(128)}, u32[]{:S(2)}) copy-start(f32[128]{0:T(128)} %param.30) | copy-start | bytes 1540
  171.1 13.0 %all-to-all-start.3 = ((bf16[4,128,512]{2,1,0:T(8,128)(2,1)}), bf16[4,128,512]{2,1,0:T(8,128)(2,1)S(1)}, u32[]{:S(2)}, u32[]{:S(2)}) async-start(bf16[4,128,512]{2,1,0:T(8,128)(2,1)} %pack_2.1), calls=%async_computation.3 | async-start | bytes 1048576 | tf_op jit(solution)/shard_map/all_to_all | solution.py:391
  184.1 0.8 copy-start.3
  224.1 18.7 %all-to-all-start.4 = ((bf16[4,256,512]{2,1,0:T(8,128)(2,1)}), bf16[4,256,512]{2,1,0:T(8,128)(2,1)S(1)}, u32[]{:S(2)}, u32[]{:S(2)}) async-start(bf16[4,256,512]{2,1,0:T(8,128)(2,1)} %pack_3.1), calls=%async_computation.4 | async-start | bytes 2097152 | tf_op jit(solution)/shard_map/all_to_all | solution.py:391
  227.6 51.3 %copy-start.5 = (f32[256]{0:T(256)S(1)}, f32[256]{0:T(256)}, u32[]{:S(2)}) copy-start(f32[256]{0:T(256)} %param.31) | copy-start | bytes 3076
  242.7 1.0 copy-start.1
  275.4 13.0 %all-to-all-start.5 = ((bf16[4,128,512]{2,1,0:T(8,128)(2,1)}), bf16[4,128,512]{2,1,0:T(8,128)(2,1)S(1)}, u32[]{:S(2)}, u32[]{:S(2)}) async-start(bf16[4,128,512]{2,1,0:T(8,128)(2,1)} %pack_4.1), calls=%async_computation.5 | async-start | bytes 1048576 | tf_op jit(solution)/shard_map/all_to_all | solution.py:391
  288.3 0.8 copy-start.2

commit v2 on v1

v2 whole, which is shorter than its diff:
```python
import functools

import jax
import jax.numpy as jnp
import numpy as np
from jax import lax
from jax.experimental import pallas as pl
from jax.experimental.pallas import tpu as pltpu
from jax.sharding import PartitionSpec as P

EPSILON = 1e-06
MESH = pl.DeviceIdType.MESH
BF16, F32, I32 = jnp.bfloat16, jnp.float32, jnp.int32
RING = 4
CORES = 2
VMEM_LIMIT = 60 * 1024 * 1024
DIRECTIONS = [
    (a, b, c) for a in (-1, 0, 1) for b in (-1, 0, 1) for c in (-1, 0, 1) if (a, b, c) != (0, 0, 0)
]


def face_sources():
    ids = np.arange(512).reshape(8, 8, 8)
    layers = [ids[7], ids[0], ids[:, 7], ids[:, 0], ids[:, :, 7], ids[:, :, 0]]
    return np.stack(layers).reshape(1, 384).astype(np.int32)


FACES = [t for t in DIRECTIONS if sum(map(abs, t)) == 1]
FACES = [FACES[0], FACES[5], FACES[1], FACES[4], FACES[2], FACES[3]]
CORNERS = [t for t in DIRECTIONS if sum(map(abs, t)) > 1]


def halo_cells():
    cells = []
    for t in FACES + CORNERS:
        spans = [(0,) if s < 0 else (9,) if s > 0 else range(1, 9) for s in t]
        cells += [(x, y, z) for x in spans[0] for y in spans[1] for z in spans[2]]
    return cells


def corner_sources():
    out = np.full((1, 128), -1, np.int32)
    for n, cell in enumerate(halo_cells()[384:]):
        t = tuple(-1 if v == 0 else 1 if v == 9 else 0 for v in cell)
        lead = next(p for p in range(3) if t[p] != 0)
        u, v = [7 if t[p] < 0 else 0 if t[p] > 0 else cell[p] - 1 for p in range(3) if p != lead]
        out[0, n] = CORNERS.index(t) * 64 + u * 8 + v
    return out


def padded_sources():
    out = np.full((1, 1280), -1, np.int32)
    halo = {cell: n for n, cell in enumerate(halo_cells())}
    for x in range(10):
        for y in range(10):
            for z in range(10):
                if (x, y, z) in halo:
                    source = 512 + halo[x, y, z]
                else:
                    source = (x - 1) * 64 + (y - 1) * 8 + z - 1
                out[0, x * 128 + y * 10 + z] = source
    return out


def shift_sources():
    out = np.zeros((9, 2, 8, 8), np.int32)
    for d in range(9):
        for q in range(2):
            for y in range(8):
                for z in range(8):
                    out[d, q, y, z] = q * 128 + (y + d // 3) * 10 + z + d % 3
    return out.reshape(1, 1152)


def octant_sources():
    out = np.zeros((8, 8, 8), np.int32)
    for x in range(8):
        for y in range(8):
            for z in range(8):
                octant = 4 * (x // 4) + 2 * (y // 4) + z // 4
                out[x, y, z] = octant * 64 + (x % 4) * 16 + (y % 4) * 4 + z % 4
    return out.reshape(1, 512)


def selection(depth, sources):
    rows = lax.broadcasted_iota(I32, (depth, sources.shape[1]), 0)
    return jnp.where(rows == sources, 1.0, 0.0).astype(BF16)


def mm(a, b):
    return jnp.dot(a, b, preferred_element_type=F32)


def as_column(row):
    size = row.shape[1]
    square = lax.broadcasted_iota(I32, (size, size), 0) == lax.broadcasted_iota(I32, (size, size), 1)
    return jnp.sum(jnp.where(square, row, 0.0), axis=1, keepdims=True)


def activate(values, gain):
    mean_sq = jnp.mean(values * values, axis=0, keepdims=True)
    scaled = values * lax.rsqrt(mean_sq + EPSILON) * gain
    return (scaled / (1.0 + jnp.exp(-scaled))).astype(BF16)


def write_faces(bricks, channels, active_ref, sources_ref, table_ref):
    faces = mm(active_ref[...], selection(512, sources_ref[...])).astype(BF16)
    for b in range(bricks):
        for pair in range(3):
            table_ref[3 * b + pair] = faces[
                b * channels : (b + 1) * channels, pair * 128 : (pair + 1) * 128
            ]


def enter_fine(
    bricks,
    channels,
    hidden_ref,
    gain_ref,
    sources_ref,
    *refs,
):
    sends, links = refs[:5], refs[5:10]
    active_ref, table_ref, owed_ref, asked_ref = refs[10:]
    row = 0
    for ref in sends:
        for part in range(ref.shape[1] // 128):
            owed_ref[row : row + 1] = ref[0:1, part * 128 : (part + 1) * 128]
            row += 1
    asked_ref[...] = jnp.zeros(asked_ref.shape, I32)
    row = 0
    for ref in links:
        for b in range(ref.shape[0]):
            lane = row % LINK_ROWS * 32
            asked_ref[row // LINK_ROWS, lane : lane + ref.shape[1]] = ref[b]
            row += 1
    gain = as_column(gain_ref[...])
    for b in range(bricks):
        rows = slice(b * channels, (b + 1) * channels)
        active_ref[rows] = activate(hidden_ref[rows].astype(F32), gain)
    write_faces(bricks, channels, active_ref, sources_ref, table_ref)


def enter_coarser(
    bricks, below, channels, grid_ref, lift_ref, gain_ref, sources_ref, hidden_ref, active_ref, table_ref
):
    gain = as_column(gain_ref[...])
    for b in range(bricks):
        own = slice(b * below, (b + 1) * below)
        rows = slice(b * channels, (b + 1) * channels)
        hidden = lax.dot_general(
            lift_ref[...], grid_ref[own], (((0,), (0,)), ((), ())), preferred_element_type=F32
        ).astype(BF16)
        hidden_ref[rows] = hidden
        active_ref[rows] = activate(hidden.astype(F32), gain)
    write_faces(bricks, channels, active_ref, sources_ref, table_ref)


def tile_of(index_ref, index_row, lane, table_ref):
    row = jnp.clip(index_ref[index_row, lane], 0, 2 * table_ref.shape[0] - 2)
    return table_ref[lax.shift_right_logical(row, 1)], row & 1


def either_half(half, tile, low, want):
    turned = jnp.concatenate([tile[:, 64:], tile[:, :64]], axis=1)
    return jnp.where(half == want, tile, turned)


def pack_halo(bricks, channels, index_ref, dest, base, table_ref, out_ref, gathered_ref, choose):
    lanes = lax.broadcasted_iota(I32, (channels, 128), 1)
    low = lanes < 64
    upper = jnp.where(low, 0, 1)
    order = [DIRECTIONS.index(t) for t in FACES]
    rest = [DIRECTIONS.index(t) for t in CORNERS]

    def brick(b, carry):
        rows = pl.ds(pl.multiple_of(b * channels, channels), channels)
        line = base + b
        index_row, lane = dest * LINK_ROWS + line // LINK_ROWS, line % LINK_ROWS * 32
        for pair in range(3):
            one, first = tile_of(index_ref, index_row, lane + order[2 * pair], table_ref)
            two, second = tile_of(index_ref, index_row, lane + order[2 * pair + 1], table_ref)
            one = either_half(first, one, low, 0)
            two = either_half(second, two, low, 1)
            out_ref[rows, pair * 128 : (pair + 1) * 128] = jnp.where(low, one, two)
        for n, way in enumerate(rest):
            tile, half = tile_of(index_ref, index_row, lane + way, table_ref)
            gathered_ref[rows, n * 128 : (n + 1) * 128] = jnp.where(
                upper == half, tile, jnp.zeros_like(tile)
            )
        return carry

    lax.fori_loop(0, bricks, brick, 0)
    out_ref[:, 384:512] = mm(gathered_ref[...], choose).astype(BF16)


def pack_octants(bricks, channels, index_ref, dest, base, table_ref, out_ref, gathered_ref, choose):
    low = lax.broadcasted_iota(I32, (channels, 128), 1) < 64
    for b in range(bricks):
        rows = slice(b * channels, (b + 1) * channels)
        line = base + b
        index_row, lane = dest * LINK_ROWS + line // LINK_ROWS, line % LINK_ROWS * 32
        for way in range(0, 8, 2):
            one, first = tile_of(index_ref, index_row, lane + way, table_ref)
            two, second = tile_of(index_ref, index_row, lane + way + 1, table_ref)
            one = either_half(first, one, low, 0)
            two = either_half(second, two, low, 1)
            gathered_ref[rows, way * 64 : way * 64 + 128] = jnp.where(low, one, two)
    out_ref[...] = mm(gathered_ref[...], choose).astype(BF16)


def leave(
    bricks,
    channels,
    pooled,
    active_ref,
    halo_ref,
    hidden_ref,
    kernel_ref,
    place_ref,
    shift_ref,
    out_ref,
    *rest,
):
    if pooled:
        table_ref, rest = rest[0], rest[1:]
    source_ref, padded_ref, shifts_ref, weight_ref, moved_ref = rest
    source_ref[:, 0:512] = active_ref[...]
    source_ref[:, 512:1024] = halo_ref[...]
    padded_ref[...] = mm(source_ref[...], selection(1024, place_ref[...])).astype(BF16)
    shifts_ref[...] = selection(256, shift_ref[...])
    for dx in range(3):
        for d in range(9):
            weight_ref[
                dx * channels : (dx + 1) * channels, d * channels : (d + 1) * channels
            ] = kernel_ref[dx * 9 + d]

    def brick(b, carry):
        start = b * channels if isinstance(b, int) else pl.multiple_of(b * channels, channels)
        rows = pl.ds(start, channels)
        planes = jnp.concatenate(
            [padded_ref[rows, pair * 256 : (pair + 1) * 256] for pair in range(5)], axis=0
        )
        moved = mm(planes, shifts_ref[...]).astype(BF16)
        for pair in range(5):
            for d in range(9):
                moved_ref[d * channels : (d + 1) * channels, pair * 128 : (pair + 1) * 128] = moved[
                    pair * channels : (pair + 1) * channels, d * 128 : (d + 1) * 128
                ]
        total = hidden_ref[rows].astype(F32)
        for dx in range(3):
            part = mm(weight_ref[dx * channels : (dx + 1) * channels], moved_ref[...])
            total = total + part[:, dx * 64 : dx * 64 + 512]
        out_ref[rows] = total.astype(BF16)
        return carry

    if bricks > 1:
        lax.fori_loop(0, bricks, brick, 0)
    else:
        brick(0, 0)
    if pooled:
        voxel = lax.broadcasted_iota(I32, (512, 64), 0)
        block = (
            lax.shift_left(lax.shift_right_logical(voxel, 7), 4)
            + lax.shift_left(lax.shift_right_logical(voxel, 4) & 3, 2)
            + (lax.shift_right_logical(voxel, 1) & 3)
        )
        column = lax.broadcasted_iota(I32, (512, 64), 1)
        average = jnp.where(block == column, 0.125, 0.0).astype(BF16)
        blocks = mm(out_ref[...], average).astype(BF16)
        for b in range(bricks):
            table_ref[b // 2, :, (b % 2) * 64 : (b % 2) * 64 + 64] = blocks[
                b * channels : (b + 1) * channels
            ]


def shape(*dims, dtype=BF16):
    return jax.ShapeDtypeStruct(dims, dtype)


def whole(count):
    return [pl.BlockSpec(memory_space=pltpu.VMEM)] * count


PARAMS = pltpu.CompilerParams(vmem_limit_bytes=VMEM_LIMIT)


def place_self():
    across, along = lax.axis_index("gx"), lax.axis_index("gy")
    return across // CORES, across % CORES, along // RING, along % RING


SEND_ROWS = 16
LINK_ROWS = 4
MEMBERS = RING * RING * CORES


def link_constants(steps):
    out = np.zeros((3, 8, 128), np.int32)
    row, position = 0, 0
    for bricks, width, slots in steps:
        for _ in range(bricks):
            lane = row % LINK_ROWS * 32
            out[:, row // LINK_ROWS, lane : lane + 32] = np.array(
                [width, slots.bit_length() - 1, position]
            )[:, None]
            row += 1
        position += slots * MEMBERS * RING
    return out


def resolve(found_ref, links_ref, sends_ref, constants_ref):
    y, core, x, z = place_self()
    own = (y * CORES + core) * RING + z
    sends = sends_ref[...].reshape(MEMBERS * SEND_ROWS, 128).astype(F32).astype(BF16)
    depth = lax.broadcasted_iota(I32, (MEMBERS * SEND_ROWS, 128), 0)
    across = lax.broadcasted_iota(I32, (128, 128), 0)
    for there in range(RING):
        dest = (y * CORES + core) * (RING * RING) + there * RING + z
        for r in range(LINK_ROWS):
            row = links_ref[there, r : r + 1]
            width, log, position = [constants_ref[n, r : r + 1] for n in range(3)]
            remote = row - width
            owner = lax.shift_right_arithmetic(remote, log)
            slot = remote - lax.shift_left(owner, log)
            member = lax.shift_right_arithmetic(owner, 4) * RING + (owner & 3)
            here = (
                (remote >= 0)
                & (owner < MEMBERS * RING)
                & ((lax.shift_right_arithmetic(owner, 2) & 3) == x)
            )
            place = position + lax.shift_left(jnp.full_like(row, dest), log) + slot
            line = jnp.where(here, member * SEND_ROWS + lax.shift_right_logical(place, 7), -1)
            hit = jnp.where(depth == line, 1.0, 0.0).astype(BF16)
            lines = lax.dot_general(
                sends, hit, (((0,), (0,)), ((), ())), preferred_element_type=F32
            )
            picked = jnp.sum(
                jnp.where(across == (place & 127), lines, 0.0), axis=0, keepdims=True
            ).astype(I32)
            found = jnp.where(here & (picked >= 0), member * width + picked, MEMBERS * width)
            mine = (remote < 0) & (jnp.full_like(row, there) == x)
            n = there * LINK_ROWS + r
            found_ref[n : n + 1] = jnp.where(mine, own * width + row, found)


def trade_kernel(bricks, channels, rows, halo, first, base, *refs):
    if first:
        own_ref, sources_ref, sends_ref, links_ref, constants_ref, out_ref, index_ref = refs[:7]
        refs = refs[7:]
    else:
        own_ref, sources_ref, index_ref, out_ref = refs[:4]
        refs = refs[4:]
    all_ref, parts_ref, stage_ref, come_ref, gathered_ref, send_sems, recv_sems, local_sems = refs[:8]
    y, core, x, z = place_self()
    half = channels // 2

    def at(dy, dx, dz, new_core):
        return (((y + dy) % RING) * CORES + new_core, ((x + dx) % RING) * RING + (z + dz) % RING)

    def peer(dy, dz):
        return at(dy, 0, dz, core)

    def block(dy, dz, other=False):
        new_core = 1 - core if other else core
        member = (((y + dy) % RING) * CORES + new_core) * RING + (z + dz) % RING
        return pl.ds(member * rows, rows)

    other_core = at(0, 0, 0, 1 - core)
    along_x = [at(0, k, 0, core) for k in (1, 2, 3)]
    plane = [
        (at(dy, 0, dz, 1 - core if flip else core), dy, dz, flip)
        for dy in range(RING)
        for dz in range(RING)
        for flip in (False, True)
        if (dy, dz, flip) != (0, 0, False)
    ]
    barrier = pltpu.get_barrier_semaphore()
    neighbours = [peer(1, 0), peer(3, 0), peer(0, 1), peer(0, 3), other_core]
    greeted = ([p[0] for p in plane] if first else neighbours) + along_x
    for device in greeted:
        pl.semaphore_signal(barrier, inc=1, device_id=device, device_id_type=MESH)
    all_ref[block(0, 0)] = own_ref[...]
    all_ref[MEMBERS * rows] = jnp.zeros((channels, 128), BF16)
    pl.semaphore_wait(barrier, len(greeted))

    started = []

    def remote(source, target, device):
        n = len(started)
        copy = pltpu.make_async_remote_copy(
            src_ref=source,
            dst_ref=target,
            send_sem=send_sems.at[n],
            recv_sem=recv_sems.at[n],
            device_id=device,
            device_id_type=MESH,
        )
        copy.start()
        started.append(copy)
        return n

    def landed(n, view):
        pltpu.make_async_remote_copy(
            src_ref=view,
            dst_ref=view,
            send_sem=send_sems.at[n],
            recv_sem=recv_sems.at[n],
            device_id=other_core,
            device_id_type=MESH,
        ).wait_recv()

    def send(dy, dz, start, size, device):
        part = pl.ds(start, size)
        source = own_ref.at[:, part] if (dy, dz) == (0, 0) else all_ref.at[block(dy, dz), part]
        return remote(source, all_ref.at[block(dy, dz), part], device)

    siblings = []

    def sibling(dy, dz, start, size):
        siblings.append((send(dy, dz, start, size, other_core), dy, dz, start, size))

    UP, DOWN = 1, 3

    def off(axis, k):
        return (k % RING, 0) if axis == "y" else (0, k % RING)

    def both(axis, dy, dz, start, size):
        events = []
        for step in (UP, DOWN):
            sy, sz = off(axis, step)
            n = send(dy, dz, start, size, peer(sy, sz))
            events.append((n, axis, step, (dy - sy) % RING, (dz - sz) % RING, start, size))
        return events

    def relay(event):
        n, axis, step, dy, dz, start, size = event
        piece = size // 2
        begin = start if step == UP else start + piece
        sy, sz = off(axis, step)
        m = send(dy, dz, begin, piece, peer(sy, sz))
        return (m, axis, step, (dy - sy) % RING, (dz - sz) % RING, begin, piece)

    def wait(event):
        n, _, _, dy, dz, start, size = event
        landed(n, all_ref.at[block(dy, dz), pl.ds(start, size)])

    if first:
        all_sends, all_links, found_ref = refs[8:]
        tables = []
        own_member = (y * CORES + core) * RING + z
        for device, dy, dz, flip in plane:
            n = remote(sends_ref, all_sends.at[own_member], device)
            back = (((y - dy) % RING) * CORES + (1 - core if flip else core)) * RING + (z - dz) % RING
            tables.append((n, all_sends.at[back]))
        for k, device in zip((1, 2, 3), along_x):
            n = remote(links_ref, all_links.at[x], device)
            tables.append((n, all_links.at[(x - k) % RING]))
        all_sends[own_member] = sends_ref[...]
        all_links[x] = links_ref[...]

    axes = [("z", "y", 0), ("y", "z", half)]
    ahead = [both(axis, 0, 0, start, half) for axis, _, start in axes]
    second = []
    for _, axis, start in axes:
        second += both(axis, 0, 0, start, half)
    sibling(0, 0, 0, channels)

    relays = []
    for (_, axis, start), events in zip(axes, ahead):
        passed = []
        for event in events:
            wait(event)
            passed.append(relay(event))
            second += both(axis, event[3], event[4], start, half)
            sibling(event[3], event[4], start, half)
        relays.append(passed)
    for (_, axis, start), passed in zip(axes, relays):
        for event in passed:
            wait(event)
        dy, dz = passed[0][3:5]
        second += both(axis, dy, dz, start, half)
        sibling(dy, dz, start, half)

    def settle():
        last = []
        for event in second:
            wait(event)
            last.append(relay(event))
            sibling(*event[3:])
        for event in last:
            wait(event)
            sibling(*event[3:])
        for n, dy, dz, start, size in siblings:
            landed(n, all_ref.at[block(dy, dz, True), pl.ds(start, size)])

    if first:
        for n, view in tables:
            landed(n, view)
        resolve(found_ref, all_links, all_sends, constants_ref)

    lane = sources_ref[...]
    if halo:
        depth = len(CORNERS) * 128
        at_row = lax.broadcasted_iota(I32, (depth, 128), 0)
        at_row = lax.shift_left(lax.shift_right_logical(at_row, 7), 6) + (at_row & 63)
        choose = jnp.where(at_row == lane, 1.0, 0.0).astype(BF16)
        packer = pack_halo
    else:
        choose = selection(512, lane)
        packer = pack_octants
    settle()
    if first:
        tell = pltpu.make_async_copy(found_ref, index_ref, local_sems.at[0])
        tell.start()
        tell.wait()

    size = bricks * channels
    low, high = pl.ds(0, size // 2), pl.ds(size // 2, size // 2)

    def pack(k):
        packer(
            bricks,
            channels,
            index_ref,
            (x + k) % RING,
            base,
            all_ref,
            parts_ref.at[k],
            gathered_ref,
            choose,
        )

    up, down = along_x[0], along_x[2]
    pack(2)
    pack(1)
    far_up = remote(parts_ref.at[2, low], stage_ref.at[low], up)
    far_down = remote(parts_ref.at[2, high], stage_ref.at[high], down)
    pack(3)
    near_up = [remote(parts_ref.at[1, high], come_ref.at[0, high], up)]
    pack(0)
    near_down = [remote(parts_ref.at[3, low], come_ref.at[1, low], down)]
    landed(far_up, stage_ref.at[low])
    parts_ref[1, low] = (parts_ref[1, low].astype(F32) + stage_ref[low].astype(F32)).astype(BF16)
    landed(far_down, stage_ref.at[high])
    parts_ref[3, high] = (parts_ref[3, high].astype(F32) + stage_ref[high].astype(F32)).astype(BF16)
    near_up.append(remote(parts_ref.at[1, low], come_ref.at[0, low], up))
    near_down.append(remote(parts_ref.at[3, high], come_ref.at[1, high], down))
    landed(near_up[0], come_ref.at[0, high])
    landed(near_down[0], come_ref.at[1, low])
    landed(near_up[1], come_ref.at[0, low])
    landed(near_down[1], come_ref.at[1, high])
    total = parts_ref[0].astype(F32) + come_ref[0].astype(F32) + come_ref[1].astype(F32)
    out_ref[...] = total.astype(BF16)
    for copy in started:
        copy.wait_send()


COPIES = 79 + 34 + 6


def trade(table, number, bricks, sources, halo, base, index=None, tables=None):
    rows, channels = table.shape[0], table.shape[1]
    first = index is None
    size = bricks * channels
    vmem, smem = pl.BlockSpec(memory_space=pltpu.VMEM), pl.BlockSpec(memory_space=pltpu.SMEM)
    outs, out_specs = [shape(size, 512)], [vmem]
    scratch = [
        pltpu.VMEM((MEMBERS * rows + 1, channels, 128), BF16),
        pltpu.VMEM((RING, size, 512), BF16),
        pltpu.VMEM((size, 512), BF16),
        pltpu.VMEM((2, size, 512), BF16),
        pltpu.VMEM((size, len(CORNERS) * 128 if halo else 512), BF16),
        pltpu.SemaphoreType.DMA((COPIES,)),
        pltpu.SemaphoreType.DMA((COPIES,)),
        pltpu.SemaphoreType.DMA((1,)),
    ]
    if first:
        operands, in_specs = (table, sources) + tables, [vmem] * 5
        outs.append(shape(RING * LINK_ROWS, 128, dtype=I32))
        out_specs.append(smem)
        scratch += [
            pltpu.VMEM((MEMBERS, SEND_ROWS, 128), I32),
            pltpu.VMEM((RING, 8, 128), I32),
            pltpu.VMEM((RING * LINK_ROWS, 128), I32),
        ]
    else:
        operands, in_specs = (table, sources, index), [vmem, vmem, smem]
    return pl.pallas_call(
        functools.partial(trade_kernel, bricks, channels, rows, halo, first, base),
        out_shape=outs,
        in_specs=in_specs,
        out_specs=out_specs,
        scratch_shapes=scratch,
        compiler_params=pltpu.CompilerParams(
            collective_id=number, has_side_effects=True, vmem_limit_bytes=VMEM_LIMIT
        ),
        name=f"trade_{number}",
    )(*operands)


def convolve(active, halo, hidden, kernel, bricks, pooled):
    channels = kernel.shape[1]
    outs = [shape(bricks * channels, 512)]
    if pooled:
        outs.append(shape(bricks // 2, channels, 128))
    return pl.pallas_call(
        functools.partial(leave, bricks, channels, pooled),
        out_shape=outs,
        in_specs=whole(6),
        out_specs=whole(len(outs)),
        scratch_shapes=[
            pltpu.VMEM((bricks * channels, 1024), BF16),
            pltpu.VMEM((bricks * channels, 1280), BF16),
            pltpu.VMEM((256, 1152), BF16),
            pltpu.VMEM((3 * channels, 9 * channels), BF16),
            pltpu.VMEM((9 * channels, 640), BF16),
        ],
        compiler_params=PARAMS,
        name=f"convolve_{channels}",
    )(active, halo, hidden, kernel, jnp.asarray(padded_sources()), jnp.asarray(shift_sources()))


def per_device(
    voxels_fine,
    gain_fine,
    gain_middle,
    gain_coarse,
    kernel_fine,
    kernel_middle,
    kernel_coarse,
    lift_middle,
    lift_coarse,
    links_fine,
    links_middle,
    links_coarse,
    sends_fine,
    sends_middle,
    sends_coarse,
    parents_middle,
    parents_coarse,
    uplinks_middle,
    uplinks_coarse,
):
    members = lax.axis_size("gx") * lax.axis_size("gy")
    bricks = [voxels_fine.shape[0], links_middle.shape[0], links_coarse.shape[0]]
    widths = [6 * bricks[0], 6 * bricks[1], 6 * bricks[2], bricks[0], bricks[1]]
    links = [links_fine, links_middle, links_coarse, parents_middle, parents_coarse]
    sends = [sends_fine, sends_middle, sends_coarse, uplinks_middle, uplinks_coarse]
    slots = [s.shape[1] // members for s in sends]
    rows = [t.shape[0] for t in links]
    bases = [sum(rows[:n]) for n in range(5)]
    constants = jnp.asarray(link_constants(tuple(zip(rows, widths, slots))))

    faces, corners, octants = (
        jnp.asarray(face_sources()),
        jnp.asarray(corner_sources()),
        jnp.asarray(octant_sources()),
    )
    channels = [kernel_fine.shape[1], kernel_middle.shape[1], kernel_coarse.shape[1]]
    gains = [g.reshape(1, -1) for g in (gain_fine, gain_middle, gain_coarse)]

    hidden = voxels_fine.reshape(bricks[0] * channels[0], 512)
    active, table, owed, asked = pl.pallas_call(
        functools.partial(enter_fine, bricks[0], channels[0]),
        out_shape=[
            shape(bricks[0] * channels[0], 512),
            shape(3 * bricks[0], channels[0], 128),
            shape(SEND_ROWS, 128, dtype=I32),
            shape(8, 128, dtype=I32),
        ],
        in_specs=whole(13),
        out_specs=whole(4),
        compiler_params=PARAMS,
        name="enter_0",
    )(hidden, gains[0], faces, *sends, *links)
    kernels, lifts = (kernel_fine, kernel_middle, kernel_coarse), (None, lift_middle, lift_coarse)
    outputs = []
    index = None
    for level in range(3):
        if level:
            grid = trade(
                pooled_table, 2 * level, bricks[level], octants, False, bases[2 + level], index
            )[0]
            size = bricks[level] * channels[level]
            hidden, active, table = pl.pallas_call(
                functools.partial(enter_coarser, bricks[level], channels[level - 1], channels[level]),
                out_shape=[
                    shape(size, 512),
                    shape(size, 512),
                    shape(3 * bricks[level], channels[level], 128),
                ],
                in_specs=whole(4),
                out_specs=whole(3),
                compiler_params=PARAMS,
                name=f"enter_{level}",
            )(grid, lifts[level].T, gains[level], faces)
        if level:
            halo = trade(table, 2 * level + 1, bricks[level], corners, True, bases[level], index)[0]
        else:
            halo, index = trade(
                table, 1, bricks[0], corners, True, 0, tables=(owed, asked, constants)
            )
        results = convolve(active, halo, hidden, kernels[level], bricks[level], level < 2)
        outputs.append(results[0].reshape(bricks[level], channels[level], 512))
        pooled_table = results[1] if level < 2 else None
    return tuple(outputs)


def solution(mesh):
    split = ("gx", "gy")
    placed = (P(split, None, None),) + (P(),) * 8 + (P(split, None),) * 10
    return jax.shard_map(
        per_device,
        mesh=mesh,
        in_specs=placed,
        out_specs=(P(split, None, None),) * 3,
        check_vma=False,
    )
```

time: 355 us -> 251 us (0.71)
  waiting for transfers between devices: 58.2 us -> 0 us
  Pallas kernels: 217 us -> 249 us
  starting transfers between devices: 30 us -> 0 us
  blocking collectives: 19.2 us -> 0 us
  local copies, waits for them, and re-layouts: 16 us -> 1.57 us
  other arithmetic: 12.3 us -> 0 us
    all_to_all x6 -> x0, waiting for transfers between devices: 58.2 us -> none  [the longest x5 54.9 us: swap_along_x(): lax.all_to_all(parts, 'gy', split_axis=0, concat_axis=0, tiled=True, axis...]
    pallas_call x10 -> x5, Pallas kernels: 184 us -> 217 us  [trade(): pl.pallas_call(functools.partial(trade_kernel, bricks, channels, rows, ha...]
    all_to_all x6 -> x0, starting transfers between devices: 30 us -> none  [the longest x5 18.5 us: swap_along_x(): lax.all_to_all(parts, 'gy', split_axis=0, concat_axis=0, tiled=True, axis...]
    all_to_all x1 -> x0, blocking collectives: 19.2 us -> none  [swap_along_x(): lax.all_to_all(parts, 'gy', split_axis=0, concat_axis=0, tiled=True, axis...]
    reshape x13 -> x0, local copies, waits for them, and re-layouts: 7.94 us -> none  [the longest x5 3.2 us: rows_here(): return jnp.where(here, found, members * width).reshape(-1).astype(I32)]
    unnamed x3 -> x0, other arithmetic: 4.04 us -> none
    unnamed x17 -> x1, local copies, waits for them, and re-layouts: 5.16 us -> 1.57 us
  transfers between devices with their start and end apart: 6 -> 0, of which waited for: 5 -> 0; matrix products, arithmetic and copies ran while one was open for 4% -> 0% of each run, Pallas kernels for 12% -> 0%
where the time goes in v2:
time: 251 us
  Pallas kernels  249 us (99%)
    pallas_call x5, Pallas kernels, trade(): pl.pallas_call(functools.partial(trade_kernel, bricks, channels, rows, ha...  217 us
    pallas_call x3, Pallas kernels, convolve(): pl.pallas_call(functools.partial(leave, bricks, channels, pooled), out_sh...  24.4 us

profile of v2, /device:TPU:1, one launch (start us, length us, event | category | flops | bytes accessed | tf_op | source)
XLA Modules:
  0.0 250.9 jit_solution(17944177571084015139)
XLA Ops:
  0.6 1.6 copy.32
  2.2 2.6 %enter_0.1 = (bf16[512,512]{1,0:T(8,128)(2,1)}, bf16[24,64,128]{2,1,0:T(8,128)(2,1)}, s32[16,128]{1,0:T(8,128)}, s32[8,128]{1,0:T(8,128)}) custom-call(bf16[512,512]{1,0:T(8,128)(2,1)} %bitcast.9, f32[1,64]{1,0:T(1,128)} %bitcast.16, s32[1,384]{1,0:T(1,128)} %constant.13.clone.sources_ref, s32[1,1024]{1,0:T(1,128)} %refs_0_.1, s32[1,512]{1,0:T(1,128)} %refs_1_.6, ...), custom_call_target="tpu_custom_call" | custom-call | tf_op jit(solution)/shard_map/enter_0/pallas_call | solution.py:664
  4.8 78.4 %trade_1.1 = (bf16[512,512]{1,0:T(8,128)(2,1)}, s32[16,128]{1,0:T(8,128)}) custom-call(bf16[24,64,128]{2,1,0:T(8,128)(2,1)} %get-tuple-element.20.refs_0_, s32[1,128]{1,0:T(1,128)} %constant.14.clone.refs_1_, s32[16,128]{1,0:T(8,128)} %get-tuple-element.21.refs_2_, s32[8,128]{1,0:T(8,128)} %get-tuple-element.22.refs_3_, s32[3,8,128]{2,1,0:T(8,128)} %constant.12.clone.refs_4_), custom_call_target="tpu_custom_call" | custom-call | tf_op jit(solution)/shard_map/trade_1/pallas_call | solution.py:589
  83.2 11.0 %convolve_64.1 = (bf16[512,512]{1,0:T(8,128)(2,1)}, bf16[4,64,128]{2,1,0:T(8,128)(2,1)}) custom-call(bf16[512,512]{1,0:T(8,128)(2,1)} %get-tuple-element.19.active_ref, bf16[512,512]{1,0:T(8,128)(2,1)} %get-tuple-element.23.halo_ref, bf16[512,512]{1,0:T(8,128)(2,1)} %bitcast.10, bf16[27,64,64]{2,1,0:T(8,128)(2,1)} %kernel_ref.3, ...), custom_call_target="tpu_custom_call" | custom-call | tf_op jit(solution)/shard_map/convolve_64/pallas_call | solution.py:607
  94.2 30.9 %trade_2.1.grid_ref = bf16[128,512]{1,0:T(8,128)(2,1)} custom-call(bf16[4,64,128]{2,1,0:T(8,128)(2,1)} %get-tuple-element.25.refs_0_, s32[1,512]{1,0:T(1,128)} %constant.15.clone.refs_1_, s32[16,128]{1,0:T(8,128)} %get-tuple-element.26.refs_2_), custom_call_target="tpu_custom_call" | custom-call | tf_op jit(solution)/shard_map/trade_2/pallas_call | solution.py:589
  125.1 2.3 enter_1.1
  127.4 40.8 %trade_3.1.halo_ref = bf16[256,512]{1,0:T(8,128)(2,1)} custom-call(bf16[6,128,128]{2,1,0:T(8,128)(2,1)} %get-tuple-element.28.refs_0_, s32[1,128]{1,0:T(1,128)} %constant.14.clone.refs_1_, s32[16,128]{1,0:T(8,128)} %get-tuple-element.26.refs_2_), custom_call_target="tpu_custom_call" | custom-call | tf_op jit(solution)/shard_map/trade_3/pallas_call | solution.py:589
  168.2 6.2 %convolve_128.1 = (bf16[256,512]{1,0:T(8,128)(2,1)}, bf16[1,128,128]{2,1,0:T(8,128)(2,1)}) custom-call(bf16[256,512]{1,0:T(8,128)(2,1)} %get-tuple-element.27.active_ref, bf16[256,512]{1,0:T(8,128)(2,1)} %trade_3.1.halo_ref, bf16[256,512]{1,0:T(8,128)(2,1)} %get-tuple-element.29.hidden_ref, bf16[27,128,128]{2,1,0:T(8,128)(2,1)} %kernel_ref.4, ...), custom_call_target="tpu_custom_call" | custom-call | tf_op jit(solution)/shard_map/convolve_128/pallas_call | solution.py:607
  174.4 28.0 %trade_4.1.grid_ref = bf16[128,512]{1,0:T(8,128)(2,1)} custom-call(bf16[1,128,128]{2,1,0:T(8,128)(2,1)} %get-tuple-element.31.refs_0_, s32[1,512]{1,0:T(1,128)} %constant.15.clone.refs_1_, s32[16,128]{1,0:T(8,128)} %get-tuple-element.26.refs_2_), custom_call_target="tpu_custom_call" | custom-call | tf_op jit(solution)/shard_map/trade_4/pallas_call | solution.py:589
  202.5 2.3 enter_2.1
  204.8 38.9 %trade_5.1.halo_ref = bf16[256,512]{1,0:T(8,128)(2,1)} custom-call(bf16[3,256,128]{2,1,0:T(8,128)(2,1)} %get-tuple-element.33.refs_0_, s32[1,128]{1,0:T(1,128)} %constant.14.clone.refs_1_, s32[16,128]{1,0:T(8,128)} %get-tuple-element.26.refs_2_), custom_call_target="tpu_custom_call" | custom-call | tf_op jit(solution)/shard_map/trade_5/pallas_call | solution.py:589
  243.7 7.2 %convolve_256.1 = bf16[256,512]{1,0:T(8,128)(2,1)} custom-call(bf16[256,512]{1,0:T(8,128)(2,1)} %get-tuple-element.32.active_ref, bf16[256,512]{1,0:T(8,128)(2,1)} %trade_5.1.halo_ref, bf16[256,512]{1,0:T(8,128)(2,1)} %get-tuple-element.34.hidden_ref, bf16[27,256,256]{2,1,0:T(8,128)(2,1)} %kernel_ref.5, s32[1,1280]{1,0:T(1,128)} %constant.16.clone.place_ref, ...), custom_call_target="tpu_custom_call" | custom-call | tf_op jit(solution)/shard_map/convolve_256/pallas_call | solution.py:607

commit v3 on v2

--- a/solution.py
+++ b/solution.py
@@ -13,7 +13,7 @@
 BF16, F32, I32 = jnp.bfloat16, jnp.float32, jnp.int32
 RING = 4
 CORES = 2
-VMEM_LIMIT = 60 * 1024 * 1024
+VMEM_LIMIT = 63 * 1024 * 1024
 DIRECTIONS = [
     (a, b, c) for a in (-1, 0, 1) for b in (-1, 0, 1) for c in (-1, 0, 1) if (a, b, c) != (0, 0, 0)
 ]
@@ -112,21 +112,12 @@
             ]
 
 
-def enter_fine(
-    bricks,
-    channels,
-    hidden_ref,
-    gain_ref,
-    sources_ref,
-    *refs,
-):
-    sends, links = refs[:5], refs[5:10]
-    active_ref, table_ref, owed_ref, asked_ref = refs[10:]
-    row = 0
-    for ref in sends:
-        for part in range(ref.shape[1] // 128):
-            owed_ref[row : row + 1] = ref[0:1, part * 128 : (part + 1) * 128]
-            row += 1
+def list_slots(sends, links, owed_ref, asked_ref):
+    owed_ref[...] = jnp.zeros(owed_ref.shape, I32)
+    for across in range(owed_ref.shape[0]):
+        for kind, ref in enumerate(sends):
+            part = across * ref.shape[1] // (owed_ref.shape[0] * 128)
+            owed_ref[across, kind : kind + 1] = ref[0:1, part * 128 : (part + 1) * 128]
     asked_ref[...] = jnp.zeros(asked_ref.shape, I32)
     row = 0
     for ref in links:
@@ -134,6 +125,9 @@
             lane = row % LINK_ROWS * 32
             asked_ref[row // LINK_ROWS, lane : lane + ref.shape[1]] = ref[b]
             row += 1
+
+
+def enter_fine(bricks, channels, hidden_ref, gain_ref, sources_ref, active_ref, table_ref):
     gain = as_column(gain_ref[...])
     for b in range(bricks):
         rows = slice(b * channels, (b + 1) * channels)
@@ -142,14 +136,14 @@
 
 
 def enter_coarser(
-    bricks, below, channels, grid_ref, lift_ref, gain_ref, sources_ref, hidden_ref, active_ref, table_ref
+    bricks, below, channels, turned, grid_ref, lift_ref, gain_ref, sources_ref, hidden_ref, active_ref, table_ref
 ):
     gain = as_column(gain_ref[...])
     for b in range(bricks):
         own = slice(b * below, (b + 1) * below)
         rows = slice(b * channels, (b + 1) * channels)
         hidden = lax.dot_general(
-            lift_ref[...], grid_ref[own], (((0,), (0,)), ((), ())), preferred_element_type=F32
+            lift_ref[...], grid_ref[own], (((0 if turned else 1,), (0,)), ((), ())), preferred_element_type=F32
         ).astype(BF16)
         hidden_ref[rows] = hidden
         active_ref[rows] = activate(hidden.astype(F32), gain)
@@ -209,31 +203,31 @@
     out_ref[...] = mm(gathered_ref[...], choose).astype(BF16)
 
 
-def leave(
-    bricks,
-    channels,
-    pooled,
-    active_ref,
-    halo_ref,
-    hidden_ref,
-    kernel_ref,
-    place_ref,
-    shift_ref,
-    out_ref,
-    *rest,
-):
-    if pooled:
-        table_ref, rest = rest[0], rest[1:]
-    source_ref, padded_ref, shifts_ref, weight_ref, moved_ref = rest
-    source_ref[:, 0:512] = active_ref[...]
-    source_ref[:, 512:1024] = halo_ref[...]
-    padded_ref[...] = mm(source_ref[...], selection(1024, place_ref[...])).astype(BF16)
-    shifts_ref[...] = selection(256, shift_ref[...])
+def arrange(channels, kernel_ref, weight_ref):
     for dx in range(3):
         for d in range(9):
             weight_ref[
                 dx * channels : (dx + 1) * channels, d * channels : (d + 1) * channels
             ] = kernel_ref[dx * 9 + d]
+
+
+def convolve(
+    bricks,
+    channels,
+    active_ref,
+    halo_ref,
+    hidden_ref,
+    weight_ref,
+    place_ref,
+    shifts_ref,
+    out_ref,
+    source_ref,
+    padded_ref,
+    moved_ref,
+):
+    source_ref[:, 0:512] = active_ref[...]
+    source_ref[:, 512:1024] = halo_ref[...]
+    padded_ref[...] = mm(source_ref[...], place_ref[...]).astype(BF16)
 
     def brick(b, carry):
         start = b * channels if isinstance(b, int) else pl.multiple_of(b * channels, channels)
@@ -247,10 +241,10 @@
                 moved_ref[d * channels : (d + 1) * channels, pair * 128 : (pair + 1) * 128] = moved[
                     pair * channels : (pair + 1) * channels, d * 128 : (d + 1) * 128
                 ]
+        parts = mm(weight_ref[...], moved_ref[...])
         total = hidden_ref[rows].astype(F32)
         for dx in range(3):
-            part = mm(weight_ref[dx * channels : (dx + 1) * channels], moved_ref[...])
-            total = total + part[:, dx * 64 : dx * 64 + 512]
+            total = total + parts[dx * channels : (dx + 1) * channels, dx * 64 : dx * 64 + 512]
         out_ref[rows] = total.astype(BF16)
         return carry
 
@@ -258,20 +252,22 @@
         lax.fori_loop(0, bricks, brick, 0)
     else:
         brick(0, 0)
-    if pooled:
-        voxel = lax.broadcasted_iota(I32, (512, 64), 0)
-        block = (
-            lax.shift_left(lax.shift_right_logical(voxel, 7), 4)
-            + lax.shift_left(lax.shift_right_logical(voxel, 4) & 3, 2)
-            + (lax.shift_right_logical(voxel, 1) & 3)
-        )
-        column = lax.broadcasted_iota(I32, (512, 64), 1)
-        average = jnp.where(block == column, 0.125, 0.0).astype(BF16)
-        blocks = mm(out_ref[...], average).astype(BF16)
-        for b in range(bricks):
-            table_ref[b // 2, :, (b % 2) * 64 : (b % 2) * 64 + 64] = blocks[
-                b * channels : (b + 1) * channels
-            ]
+
+
+def pool(bricks, channels, out_ref, table_ref):
+    voxel = lax.broadcasted_iota(I32, (512, 64), 0)
+    block = (
+        lax.shift_left(lax.shift_right_logical(voxel, 7), 4)
+        + lax.shift_left(lax.shift_right_logical(voxel, 4) & 3, 2)
+        + (lax.shift_right_logical(voxel, 1) & 3)
+    )
+    column = lax.broadcasted_iota(I32, (512, 64), 1)
+    average = jnp.where(block == column, 0.125, 0.0).astype(BF16)
+    blocks = mm(out_ref[...], average).astype(BF16)
+    for b in range(bricks):
+        table_ref[b // 2, :, (b % 2) * 64 : (b % 2) * 64 + 64] = blocks[
+            b * channels : (b + 1) * channels
+        ]
 
 
 def shape(*dims, dtype=BF16):
@@ -290,22 +286,21 @@
     return across // CORES, across % CORES, along // RING, along % RING
 
 
-SEND_ROWS = 16
+SEND_ROWS = 8
 LINK_ROWS = 4
 MEMBERS = RING * RING * CORES
 
 
 def link_constants(steps):
     out = np.zeros((3, 8, 128), np.int32)
-    row, position = 0, 0
-    for bricks, width, slots in steps:
+    row = 0
+    for kind, (bricks, width, slots) in enumerate(steps):
         for _ in range(bricks):
             lane = row % LINK_ROWS * 32
             out[:, row // LINK_ROWS, lane : lane + 32] = np.array(
-                [width, slots.bit_length() - 1, position]
+                [width, slots.bit_length() - 1, kind]
             )[:, None]
             row += 1
-        position += slots * MEMBERS * RING
     return out
 
 
@@ -319,7 +314,7 @@
         dest = (y * CORES + core) * (RING * RING) + there * RING + z
         for r in range(LINK_ROWS):
             row = links_ref[there, r : r + 1]
-            width, log, position = [constants_ref[n, r : r + 1] for n in range(3)]
+            width, log, kind = [constants_ref[n, r : r + 1] for n in range(3)]
             remote = row - width
             owner = lax.shift_right_arithmetic(remote, log)
             slot = remote - lax.shift_left(owner, log)
@@ -329,8 +324,8 @@
                 & (owner < MEMBERS * RING)
                 & ((lax.shift_right_arithmetic(owner, 2) & 3) == x)
             )
-            place = position + lax.shift_left(jnp.full_like(row, dest), log) + slot
-            line = jnp.where(here, member * SEND_ROWS + lax.shift_right_logical(place, 7), -1)
+            place = lax.shift_left(jnp.full_like(row, dest), log) + slot
+            line = jnp.where(here, member * SEND_ROWS + kind, -1)
             hit = jnp.where(depth == line, 1.0, 0.0).astype(BF16)
             lines = lax.dot_general(
                 sends, hit, (((0,), (0,)), ((), ())), preferred_element_type=F32
@@ -344,14 +339,42 @@
             found_ref[n : n + 1] = jnp.where(mine, own * width + row, found)
 
 
-def trade_kernel(bricks, channels, rows, halo, first, base, *refs):
-    if first:
-        own_ref, sources_ref, sends_ref, links_ref, constants_ref, out_ref, index_ref = refs[:7]
-        refs = refs[7:]
-    else:
-        own_ref, sources_ref, index_ref, out_ref = refs[:4]
-        refs = refs[4:]
-    all_ref, parts_ref, stage_ref, come_ref, gathered_ref, send_sems, recv_sems, local_sems = refs[:8]
+def greet():
+    y, core, x, z = place_self()
+    barrier = pltpu.get_barrier_semaphore()
+    devices = [
+        (((y + dy) % RING) * CORES + (1 - core if flip else core), x * RING + (z + dz) % RING)
+        for dy in range(RING)
+        for dz in range(RING)
+        for flip in (False, True)
+        if (dy, dz, flip) != (0, 0, False)
+    ]
+    devices += [(y * CORES + core, ((x + k) % RING) * RING + z) for k in (1, 2, 3)]
+    for device in devices:
+        pl.semaphore_signal(barrier, inc=1, device_id=device, device_id_type=MESH)
+    return len(devices)
+
+
+def trade(
+    bricks,
+    channels,
+    rows,
+    halo,
+    base,
+    own_ref,
+    index_ref,
+    out_ref,
+    all_ref,
+    parts_ref,
+    stage_ref,
+    come_ref,
+    gathered_ref,
+    choose_ref,
+    send_sems,
+    recv_sems,
+    tables=None,
+    meanwhile=None,
+):
     y, core, x, z = place_self()
     half = channels // 2
 
@@ -375,14 +398,8 @@
         for flip in (False, True)
         if (dy, dz, flip) != (0, 0, False)
     ]
-    barrier = pltpu.get_barrier_semaphore()
-    neighbours = [peer(1, 0), peer(3, 0), peer(0, 1), peer(0, 3), other_core]
-    greeted = ([p[0] for p in plane] if first else neighbours) + along_x
-    for device in greeted:
-        pl.semaphore_signal(barrier, inc=1, device_id=device, device_id_type=MESH)
     all_ref[block(0, 0)] = own_ref[...]
     all_ref[MEMBERS * rows] = jnp.zeros((channels, 128), BF16)
-    pl.semaphore_wait(barrier, len(greeted))
 
     started = []
 
@@ -445,19 +462,19 @@
         n, _, _, dy, dz, start, size = event
         landed(n, all_ref.at[block(dy, dz), pl.ds(start, size)])
 
-    if first:
-        all_sends, all_links, found_ref = refs[8:]
-        tables = []
+    arrivals = []
+    if tables:
+        owed_ref, asked_ref, all_sends, all_links = tables
         own_member = (y * CORES + core) * RING + z
         for device, dy, dz, flip in plane:
-            n = remote(sends_ref, all_sends.at[own_member], device)
+            n = remote(owed_ref.at[device[0]], all_sends.at[own_member], device)
             back = (((y - dy) % RING) * CORES + (1 - core if flip else core)) * RING + (z - dz) % RING
-            tables.append((n, all_sends.at[back]))
+            arrivals.append((n, all_sends.at[back]))
         for k, device in zip((1, 2, 3), along_x):
-            n = remote(links_ref, all_links.at[x], device)
-            tables.append((n, all_links.at[(x - k) % RING]))
-        all_sends[own_member] = sends_ref[...]
-        all_links[x] = links_ref[...]
+            n = remote(asked_ref, all_links.at[x], device)
+            arrivals.append((n, all_links.at[(x - k) % RING]))
+        all_sends[own_member] = owed_ref[y * CORES + core]
+        all_links[x] = asked_ref[...]
 
     axes = [("z", "y", 0), ("y", "z", half)]
     ahead = [both(axis, 0, 0, start, half) for axis, _, start in axes]
@@ -494,26 +511,12 @@
         for n, dy, dz, start, size in siblings:
             landed(n, all_ref.at[block(dy, dz, True), pl.ds(start, size)])
 
-    if first:
-        for n, view in tables:
-            landed(n, view)
-        resolve(found_ref, all_links, all_sends, constants_ref)
-
-    lane = sources_ref[...]
-    if halo:
-        depth = len(CORNERS) * 128
-        at_row = lax.broadcasted_iota(I32, (depth, 128), 0)
-        at_row = lax.shift_left(lax.shift_right_logical(at_row, 7), 6) + (at_row & 63)
-        choose = jnp.where(at_row == lane, 1.0, 0.0).astype(BF16)
-        packer = pack_halo
-    else:
-        choose = selection(512, lane)
-        packer = pack_octants
+    for n, view in arrivals:
+        landed(n, view)
+    if meanwhile:
+        meanwhile()
     settle()
-    if first:
-        tell = pltpu.make_async_copy(found_ref, index_ref, local_sems.at[0])
-        tell.start()
-        tell.wait()
+    packer = pack_halo if halo else pack_octants
 
     size = bricks * channels
     low, high = pl.ds(0, size // 2), pl.ds(size // 2, size // 2)
@@ -528,17 +531,16 @@
             all_ref,
             parts_ref.at[k],
             gathered_ref,
-            choose,
+            choose_ref[...],
         )
 
     up, down = along_x[0], along_x[2]
     pack(2)
-    pack(1)
     far_up = remote(parts_ref.at[2, low], stage_ref.at[low], up)
     far_down = remote(parts_ref.at[2, high], stage_ref.at[high], down)
+    pack(1)
+    near_up = [remote(parts_ref.at[1, high], come_ref.at[0, high], up)]
     pack(3)
-    near_up = [remote(parts_ref.at[1, high], come_ref.at[0, high], up)]
-    pack(0)
     near_down = [remote(parts_ref.at[3, low], come_ref.at[1, low], down)]
     landed(far_up, stage_ref.at[low])
     parts_ref[1, low] = (parts_ref[1, low].astype(F32) + stage_ref[low].astype(F32)).astype(BF16)
@@ -546,6 +548,7 @@
     parts_ref[3, high] = (parts_ref[3, high].astype(F32) + stage_ref[high].astype(F32)).astype(BF16)
     near_up.append(remote(parts_ref.at[1, low], come_ref.at[0, low], up))
     near_down.append(remote(parts_ref.at[3, high], come_ref.at[1, high], down))
+    pack(0)
     landed(near_up[0], come_ref.at[0, high])
     landed(near_down[0], come_ref.at[1, low])
     landed(near_up[1], come_ref.at[0, low])
@@ -559,66 +562,155 @@
 COPIES = 79 + 34 + 6
 
 
-def trade(table, number, bricks, sources, halo, base, index=None, tables=None):
-    rows, channels = table.shape[0], table.shape[1]
-    first = index is None
-    size = bricks * channels
-    vmem, smem = pl.BlockSpec(memory_space=pltpu.VMEM), pl.BlockSpec(memory_space=pltpu.SMEM)
-    outs, out_specs = [shape(size, 512)], [vmem]
-    scratch = [
-        pltpu.VMEM((MEMBERS * rows + 1, channels, 128), BF16),
-        pltpu.VMEM((RING, size, 512), BF16),
-        pltpu.VMEM((size, 512), BF16),
-        pltpu.VMEM((2, size, 512), BF16),
-        pltpu.VMEM((size, len(CORNERS) * 128 if halo else 512), BF16),
-        pltpu.SemaphoreType.DMA((COPIES,)),
-        pltpu.SemaphoreType.DMA((COPIES,)),
-        pltpu.SemaphoreType.DMA((1,)),
+def body_kernel(bricks, channels, *refs):
+    (
+        voxels, gain0, gain1, gain2, lift1, lift2, constants, faces, corners, octants, places, shifts
+    ) = refs[:12]
+    sends, links = refs[12:17], refs[17:22]
+    kernel0_hbm, kernel1_hbm = refs[22:24]
+    out0_hbm, out1_hbm, hidden2, active2, halo2 = refs[24:29]
+    (
+        owed, asked, all_sends, all_links, found, index,
+        active0, hidden1, active1, out0, out1, halo0, halo1, grid1, grid2,
+        own0, own1, own2, pooled0, pooled1,
+        kernel0, kernel1, weight0, weight1,
+        choose_corners, choose_octants, place_matrix, shift_matrix,
+        gathered, source, padded, moved,
+    ) = refs[29:61]
+    buffers = [refs[61 + 4 * n : 65 + 4 * n] for n in range(5)]
+    send_sems, recv_sems, local_sems = refs[81:]
+
+    count = greet()
+    fetch = [
+        pltpu.make_async_copy(kernel0_hbm, kernel0, local_sems.at[0]),
+        pltpu.make_async_copy(kernel1_hbm, kernel1, local_sems.at[1]),
     ]
-    if first:
-        operands, in_specs = (table, sources) + tables, [vmem] * 5
-        outs.append(shape(RING * LINK_ROWS, 128, dtype=I32))
-        out_specs.append(smem)
-        scratch += [
-            pltpu.VMEM((MEMBERS, SEND_ROWS, 128), I32),
-            pltpu.VMEM((RING, 8, 128), I32),
-            pltpu.VMEM((RING * LINK_ROWS, 128), I32),
-        ]
-    else:
-        operands, in_specs = (table, sources, index), [vmem, vmem, smem]
-    return pl.pallas_call(
-        functools.partial(trade_kernel, bricks, channels, rows, halo, first, base),
-        out_shape=outs,
-        in_specs=in_specs,
-        out_specs=out_specs,
-        scratch_shapes=scratch,
-        compiler_params=pltpu.CompilerParams(
-            collective_id=number, has_side_effects=True, vmem_limit_bytes=VMEM_LIMIT
-        ),
-        name=f"trade_{number}",
-    )(*operands)
-
-
-def convolve(active, halo, hidden, kernel, bricks, pooled):
-    channels = kernel.shape[1]
-    outs = [shape(bricks * channels, 512)]
-    if pooled:
-        outs.append(shape(bricks // 2, channels, 128))
-    return pl.pallas_call(
-        functools.partial(leave, bricks, channels, pooled),
-        out_shape=outs,
-        in_specs=whole(6),
-        out_specs=whole(len(outs)),
-        scratch_shapes=[
-            pltpu.VMEM((bricks * channels, 1024), BF16),
-            pltpu.VMEM((bricks * channels, 1280), BF16),
-            pltpu.VMEM((256, 1152), BF16),
-            pltpu.VMEM((3 * channels, 9 * channels), BF16),
-            pltpu.VMEM((9 * channels, 640), BF16),
-        ],
-        compiler_params=PARAMS,
-        name=f"convolve_{channels}",
-    )(active, halo, hidden, kernel, jnp.asarray(padded_sources()), jnp.asarray(shift_sources()))
+    for copy in fetch:
+        copy.start()
+    list_slots(sends, links, owed, asked)
+    enter_fine(bricks[0], channels[0], voxels, gain0, faces, active0, own0)
+    pl.semaphore_wait(pltpu.get_barrier_semaphore(), count)
+
+    def meanwhile():
+        resolve(found, all_links, all_sends, constants)
+        depth = len(CORNERS) * 128
+        at_row = lax.broadcasted_iota(I32, (depth, 128), 0)
+        at_row = lax.shift_left(lax.shift_right_logical(at_row, 7), 6) + (at_row & 63)
+        choose_corners[...] = jnp.where(at_row == corners[...], 1.0, 0.0).astype(BF16)
+        tell = pltpu.make_async_copy(found, index, local_sems.at[2])
+        tell.start()
+        choose_octants[...] = selection(512, octants[...])
+        shift_matrix[...] = selection(256, shifts[...])
+        tell.wait()
+        for copy in fetch:
+            copy.wait()
+        arrange(channels[0], kernel0, weight0)
+
+    def step(n, level, halo, base, own, out, **more):
+        below = channels[level] if halo else channels[level - 1]
+        size = bricks[level] * below
+        wide = len(CORNERS) * 128 if halo else 512
+        trade(
+            bricks[level],
+            below,
+            own.shape[0],
+            halo,
+            base,
+            own,
+            index,
+            out,
+            *buffers[n],
+            gathered.at[pl.ds(0, size), pl.ds(0, wide)],
+            choose_corners if halo else choose_octants,
+            send_sems.at[n % 2],
+            recv_sems.at[n % 2],
+            **more,
+        )
+
+    def leave(level, active, halo, hidden, weight, out):
+        size = bricks[level] * channels[level]
+        convolve(
+            bricks[level],
+            channels[level],
+            active,
+            halo,
+            hidden,
+            weight,
+            place_matrix,
+            shift_matrix,
+            out,
+            source.at[pl.ds(0, size)],
+            padded.at[pl.ds(0, size)],
+            moved.at[pl.ds(0, 9 * channels[level])],
+        )
+
+    lines = [0, bricks[0], bricks[0] + bricks[1], sum(bricks), sum(bricks) + bricks[1]]
+    step(
+        0, 0, True, lines[0], own0, halo0, tables=(owed, asked, all_sends, all_links), meanwhile=meanwhile
+    )
+    place_matrix[...] = selection(1024, places[...])
+    leave(0, active0, halo0, voxels, weight0, out0)
+    keep0 = pltpu.make_async_copy(out0, out0_hbm, local_sems.at[3])
+    keep0.start()
+    pool(bricks[0], channels[0], out0, pooled0)
+    step(1, 1, False, lines[3], pooled0, grid1, meanwhile=lambda: arrange(channels[1], kernel1, weight1))
+    enter_coarser(
+        bricks[1], channels[0], channels[1], True, grid1, lift1, gain1, faces, hidden1, active1, own1
+    )
+    step(2, 1, True, lines[1], own1, halo1)
+    leave(1, active1, halo1, hidden1, weight1, out1)
+    keep1 = pltpu.make_async_copy(out1, out1_hbm, local_sems.at[4])
+    keep1.start()
+    pool(bricks[1], channels[1], out1, pooled1)
+    step(3, 2, False, lines[4], pooled1, grid2)
+    enter_coarser(
+        bricks[2], channels[1], channels[2], False, grid2, lift2, gain2, faces, hidden2, active2, own2
+    )
+    step(4, 2, True, lines[2], own2, halo2)
+    keep0.wait()
+    keep1.wait()
+
+
+def last_kernel(
+    bricks,
+    channels,
+    active_ref,
+    halo_ref,
+    hidden_ref,
+    kernel_ref,
+    places_ref,
+    shifts_ref,
+    fine_ref,
+    middle_ref,
+    fine_out,
+    middle_out,
+    out_ref,
+    place_matrix,
+    shift_matrix,
+    weight_ref,
+    source_ref,
+    padded_ref,
+    moved_ref,
+):
+    fine_out[...] = fine_ref[...]
+    middle_out[...] = middle_ref[...]
+    place_matrix[...] = selection(1024, places_ref[...])
+    shift_matrix[...] = selection(256, shifts_ref[...])
+    arrange(channels, kernel_ref, weight_ref)
+    convolve(
+        bricks,
+        channels,
+        active_ref,
+        halo_ref,
+        hidden_ref,
+        weight_ref,
+        place_matrix,
+        shift_matrix,
+        out_ref,
+        source_ref,
+        padded_ref,
+        moved_ref,
+    )
 
 
 def per_device(
@@ -649,62 +741,116 @@
     sends = [sends_fine, sends_middle, sends_coarse, uplinks_middle, uplinks_coarse]
     slots = [s.shape[1] // members for s in sends]
     rows = [t.shape[0] for t in links]
-    bases = [sum(rows[:n]) for n in range(5)]
     constants = jnp.asarray(link_constants(tuple(zip(rows, widths, slots))))
 
-    faces, corners, octants = (
+    kernels = (kernel_fine, kernel_middle, kernel_coarse)
+    channels = [k.shape[1] for k in kernels]
+    sizes = [b * c for b, c in zip(bricks, channels)]
+    places, shifts = jnp.asarray(padded_sources()), jnp.asarray(shift_sources())
+    gains = [g.reshape(1, -1) for g in (gain_fine, gain_middle, gain_coarse)]
+    hidden = voxels_fine.reshape(sizes[0], 512)
+
+    def vmem(*dims, dtype=BF16):
+        return pltpu.VMEM(dims, dtype)
+
+    owns = [(3 * b, c, 128) for b, c in zip(bricks, channels)]
+    pooled = [(bricks[n] // 2, channels[n], 128) for n in range(2)]
+    grids = [bricks[n + 1] * channels[n] for n in range(2)]
+    scratch = [
+        vmem(2 * RING, SEND_ROWS, 128, dtype=I32),
+        vmem(8, 128, dtype=I32),
+        vmem(MEMBERS, SEND_ROWS, 128, dtype=I32),
+        vmem(RING, 8, 128, dtype=I32),
+        vmem(RING * LINK_ROWS, 128, dtype=I32),
+        pltpu.SMEM((RING * LINK_ROWS, 128), I32),
+        vmem(sizes[0], 512),
+        vmem(sizes[1], 512),
+        vmem(sizes[1], 512),
+        vmem(sizes[0], 512),
+        vmem(sizes[1], 512),
+        vmem(sizes[0], 512),
+        vmem(sizes[1], 512),
+        vmem(grids[0], 512),
+        vmem(grids[1], 512),
+        vmem(*owns[0]),
+        vmem(*owns[1]),
+        vmem(*owns[2]),
+        vmem(*pooled[0]),
+        vmem(*pooled[1]),
+        vmem(*kernel_fine.shape),
+        vmem(*kernel_middle.shape),
+        vmem(3 * channels[0], 9 * channels[0]),
+        vmem(3 * channels[1], 9 * channels[1]),
+        vmem(len(CORNERS) * 128, 128),
+        vmem(512, 512),
+        vmem(1024, 1280),
+        vmem(256, 1152),
+        vmem(max(sizes), len(CORNERS) * 128),
+        vmem(max(sizes[:2]), 1024),
+        vmem(max(sizes[:2]), 1280),
+        vmem(9 * channels[1], 640),
+    ]
+    for table, size in zip(
+        (owns[0], pooled[0], owns[1], pooled[1], owns[2]),
+        (sizes[0], grids[0], sizes[1], grids[1], sizes[2]),
+    ):
+        scratch += [
+            vmem(MEMBERS * table[0] + 1, table[1], 128),
+            vmem(RING, size, 512),
+            vmem(size, 512),
+            vmem(2, size, 512),
+        ]
+    scratch += [
+        pltpu.SemaphoreType.DMA((2, COPIES)),
+        pltpu.SemaphoreType.DMA((2, COPIES)),
+        pltpu.SemaphoreType.DMA((5,)),
+    ]
+    anywhere = pl.BlockSpec(memory_space=pl.ANY)
+    fine, middle, hidden, active, halo = pl.pallas_call(
+        functools.partial(body_kernel, bricks, channels),
+        out_shape=[shape(sizes[0], 512), shape(sizes[1], 512)] + [shape(sizes[2], 512)] * 3,
+        in_specs=whole(22) + [anywhere] * 2,
+        out_specs=[anywhere] * 2 + whole(3),
+        scratch_shapes=scratch,
+        compiler_params=pltpu.CompilerParams(
+            collective_id=0, has_side_effects=True, vmem_limit_bytes=VMEM_LIMIT
+        ),
+        name="levels",
+    )(
+        hidden,
+        *gains,
+        lift_middle.T,
+        lift_coarse,
+        constants,
         jnp.asarray(face_sources()),
         jnp.asarray(corner_sources()),
         jnp.asarray(octant_sources()),
+        places,
+        shifts,
+        *sends,
+        *links,
+        kernel_fine,
+        kernel_middle,
     )
-    channels = [kernel_fine.shape[1], kernel_middle.shape[1], kernel_coarse.shape[1]]
-    gains = [g.reshape(1, -1) for g in (gain_fine, gain_middle, gain_coarse)]
-
-    hidden = voxels_fine.reshape(bricks[0] * channels[0], 512)
-    active, table, owed, asked = pl.pallas_call(
-        functools.partial(enter_fine, bricks[0], channels[0]),
-        out_shape=[
-            shape(bricks[0] * channels[0], 512),
-            shape(3 * bricks[0], channels[0], 128),
-            shape(SEND_ROWS, 128, dtype=I32),
-            shape(8, 128, dtype=I32),
+    outputs = pl.pallas_call(
+        functools.partial(last_kernel, bricks[2], channels[2]),
+        out_shape=[shape(size, 512) for size in sizes],
+        in_specs=whole(8),
+        out_specs=whole(3),
+        scratch_shapes=[
+            vmem(1024, 1280),
+            vmem(256, 1152),
+            vmem(3 * channels[2], 9 * channels[2]),
+            vmem(sizes[2], 1024),
+            vmem(sizes[2], 1280),
+            vmem(9 * channels[2], 640),
         ],
-        in_specs=whole(13),
-        out_specs=whole(4),
         compiler_params=PARAMS,
-        name="enter_0",
-    )(hidden, gains[0], faces, *sends, *links)
-    kernels, lifts = (kernel_fine, kernel_middle, kernel_coarse), (None, lift_middle, lift_coarse)
-    outputs = []
-    index = None
-    for level in range(3):
-        if level:
-            grid = trade(
-                pooled_table, 2 * level, bricks[level], octants, False, bases[2 + level], index
-            )[0]
-            size = bricks[level] * channels[level]
-            hidden, active, table = pl.pallas_call(
-                functools.partial(enter_coarser, bricks[level], channels[level - 1], channels[level]),
-                out_shape=[
-                    shape(size, 512),
-                    shape(size, 512),
-                    shape(3 * bricks[level], channels[level], 128),
-                ],
-                in_specs=whole(4),
-                out_specs=whole(3),
-                compiler_params=PARAMS,
-                name=f"enter_{level}",
-            )(grid, lifts[level].T, gains[level], faces)
-        if level:
-            halo = trade(table, 2 * level + 1, bricks[level], corners, True, bases[level], index)[0]
-        else:
-            halo, index = trade(
-                table, 1, bricks[0], corners, True, 0, tables=(owed, asked, constants)
-            )
-        results = convolve(active, halo, hidden, kernels[level], bricks[level], level < 2)
-        outputs.append(results[0].reshape(bricks[level], channels[level], 512))
-        pooled_table = results[1] if level < 2 else None
-    return tuple(outputs)
+        name="last",
+    )(active, halo, hidden, kernel_coarse, places, shifts, fine, middle)
+    return tuple(
+        out.reshape(b, c, 512) for out, b, c in zip(outputs, bricks, channels)
+    )
 
 
 def solution(mesh):

time: 251 us -> 213 us (0.85)
  Pallas kernels: 249 us -> 213 us
    pallas_call x11 -> x2, Pallas kernels: 249 us -> 213 us  [the longest x1 204 us: per_device(): pl.pallas_call(functools.partial(body_kernel, bricks, channels), out_shap...]
where the time goes in v3:
time: 213 us
  Pallas kernels  213 us (100%)
    pallas_call x1, Pallas kernels, per_device(): pl.pallas_call(functools.partial(body_kernel, bricks, channels), out_shap...  204 us
    pallas_call x1, Pallas kernels, per_device(): pl.pallas_call(functools.partial(last_kernel, bricks[2], channels[2]), ou...  8.13 us

profile of v3, /device:TPU:1, one launch (start us, length us, event | category | flops | bytes accessed | tf_op | source)
XLA Modules:
  0.0 213.2 jit_solution(5723357287858463024)
XLA Ops:
  0.6 204.4 %levels.1 = (bf16[512,512]{1,0:T(8,128)(2,1)}, bf16[256,512]{1,0:T(8,128)(2,1)}, bf16[256,512]{1,0:T(8,128)(2,1)}, bf16[256,512]{1,0:T(8,128)(2,1)}, bf16[256,512]{1,0:T(8,128)(2,1)}) custom-call(bf16[512,512]{1,0:T(8,128)(2,1)} %bitcast.8, f32[1,64]{1,0:T(1,128)} %bitcast.11, f32[1,128]{1,0:T(1,128)} %bitcast.12, f32[1,256]{1,0:T(1,128)} %bitcast.10, ...), custom_call_target="tpu_custom_call" | custom-call | tf_op jit(solution)/shard_map/levels/pallas_call | solution.py:809
  205.0 8.1 %last.1 = (bf16[512,512]{1,0:T(8,128)(2,1)}, bf16[256,512]{1,0:T(8,128)(2,1)}, bf16[256,512]{1,0:T(8,128)(2,1)}) custom-call(bf16[256,512]{1,0:T(8,128)(2,1)} %get-tuple-element.11.active_ref, bf16[256,512]{1,0:T(8,128)(2,1)} %get-tuple-element.12.halo_ref, bf16[256,512]{1,0:T(8,128)(2,1)} %get-tuple-element.13.hidden_ref, bf16[27,256,256]{2,1,0:T(8,128)(2,1)} %kernel_ref.1, ...), custom_call_target="tpu_custom_call" | custom-call | tf_op jit(solution)/shard_map/last/pallas_call | solution.py:835

commit v4 on v3

--- a/solution.py
+++ b/solution.py
@@ -14,6 +14,7 @@
 RING = 4
 CORES = 2
 VMEM_LIMIT = 63 * 1024 * 1024
+CHUNKS = (1, 1, 1, 1, 1)
 DIRECTIONS = [
     (a, b, c) for a in (-1, 0, 1) for b in (-1, 0, 1) for c in (-1, 0, 1) if (a, b, c) != (0, 0, 0)
 ]
@@ -38,13 +39,53 @@
     return cells
 
 
+def slab_lanes(t):
+    lead = next(p for p in range(3) if t[p] != 0)
+    spans = [(0,) if s < 0 else (9,) if s > 0 else range(1, 9) for s in t]
+    found = []
+    for cell in [(x, y, z) for x in spans[0] for y in spans[1] for z in spans[2]]:
+        u, v = [7 if t[p] < 0 else 0 if t[p] > 0 else cell[p] - 1 for p in range(3) if p != lead]
+        found.append((u * 8 + v, cell))
+    return found
+
+
+def corner_groups():
+    groups = []
+    for t in CORNERS:
+        mine = {lane for lane, _ in slab_lanes(t)}
+        for group, taken in groups:
+            if not mine & taken:
+                group.append(t)
+                taken |= mine
+                break
+        else:
+            groups.append(([t], set(mine)))
+    return [group for group, _ in groups]
+
+
+GROUPS = corner_groups()
+KINDS = sorted({tuple(sorted(lane for lane, _ in slab_lanes(t))) for t in CORNERS})
+
+
+def kind_of(t):
+    return KINDS.index(tuple(sorted(lane for lane, _ in slab_lanes(t))))
+
+
+def kind_masks():
+    out = np.zeros((2 * len(KINDS), 16, 128), np.int32)
+    for n, lanes in enumerate(KINDS):
+        for half in range(2):
+            out[2 * n + half][:, [64 * half + lane for lane in lanes]] = 1
+    return out
+
+
 def corner_sources():
     out = np.full((1, 128), -1, np.int32)
-    for n, cell in enumerate(halo_cells()[384:]):
-        t = tuple(-1 if v == 0 else 1 if v == 9 else 0 for v in cell)
-        lead = next(p for p in range(3) if t[p] != 0)
-        u, v = [7 if t[p] < 0 else 0 if t[p] > 0 else cell[p] - 1 for p in range(3) if p != lead]
-        out[0, n] = CORNERS.index(t) * 64 + u * 8 + v
+    cells = halo_cells()[384:]
+    for n, group in enumerate(GROUPS):
+        for t in group:
+            for lane, cell in slab_lanes(t):
+                out[0, cells.index(cell)] = n * 64 + lane
     return out
 
 
@@ -150,56 +191,81 @@
     write_faces(bricks, channels, active_ref, sources_ref, table_ref)
 
 
-def tile_of(index_ref, index_row, lane, table_ref):
+LOW, HIGH, NONE = 0, 1, 2
+
+
+def write_masks(masks_ref, kinds_ref):
+    masks_ref[3:] = kinds_ref[...].astype(F32).astype(BF16)
+    lanes = lax.broadcasted_iota(I32, (16, 128), 1)
+    masks_ref[LOW] = jnp.where(lanes < 64, 1.0, 0.0).astype(BF16)
+    masks_ref[HIGH] = jnp.where(lanes < 64, 0.0, 1.0).astype(BF16)
+    masks_ref[NONE] = jnp.zeros((16, 128), BF16)
+
+
+def tile_of(index_ref, index_row, lane, table_ref, part):
     row = jnp.clip(index_ref[index_row, lane], 0, 2 * table_ref.shape[0] - 2)
-    return table_ref[lax.shift_right_logical(row, 1)], row & 1
-
-
-def either_half(half, tile, low, want):
-    turned = jnp.concatenate([tile[:, 64:], tile[:, :64]], axis=1)
-    return jnp.where(half == want, tile, turned)
-
-
-def pack_halo(bricks, channels, index_ref, dest, base, table_ref, out_ref, gathered_ref, choose):
-    lanes = lax.broadcasted_iota(I32, (channels, 128), 1)
-    low = lanes < 64
-    upper = jnp.where(low, 0, 1)
+    return table_ref[lax.shift_right_logical(row, 1), part], row & 1
+
+
+def masked(tile, mask):
+    channels = tile.shape[0]
+    return (tile.reshape(channels // 16, 16, 128) * mask[None]).reshape(channels, 128)
+
+
+def turn(tile):
+    return jnp.concatenate([tile[:, 64:], tile[:, :64]], axis=1)
+
+
+def side_by_side(one, first, two, second, masks_ref):
+    low = masked(one, masks_ref[2 * first]) + masked(turn(one), masks_ref[2 - 2 * first])
+    high = masked(two, masks_ref[2 - second]) + masked(turn(two), masks_ref[1 + second])
+    return low + high
+
+
+def pack_halo(bricks, part, index_ref, dest, base, table_ref, out_ref, gathered_ref, choose, masks_ref):
+    channels = part.size
     order = [DIRECTIONS.index(t) for t in FACES]
-    rest = [DIRECTIONS.index(t) for t in CORNERS]
 
     def brick(b, carry):
-        rows = pl.ds(pl.multiple_of(b * channels, channels), channels)
+        start = b * channels if isinstance(b, int) else pl.multiple_of(b * channels, channels)
+        rows = pl.ds(start, channels)
         line = base + b
         index_row, lane = dest * LINK_ROWS + line // LINK_ROWS, line % LINK_ROWS * 32
         for pair in range(3):
-            one, first = tile_of(index_ref, index_row, lane + order[2 * pair], table_ref)
-            two, second = tile_of(index_ref, index_row, lane + order[2 * pair + 1], table_ref)
-            one = either_half(first, one, low, 0)
-            two = either_half(second, two, low, 1)
-            out_ref[rows, pair * 128 : (pair + 1) * 128] = jnp.where(low, one, two)
-        for n, way in enumerate(rest):
-            tile, half = tile_of(index_ref, index_row, lane + way, table_ref)
-            gathered_ref[rows, n * 128 : (n + 1) * 128] = jnp.where(
-                upper == half, tile, jnp.zeros_like(tile)
+            one, first = tile_of(index_ref, index_row, lane + order[2 * pair], table_ref, part)
+            two, second = tile_of(index_ref, index_row, lane + order[2 * pair + 1], table_ref, part)
+            out_ref[rows, pair * 128 : (pair + 1) * 128] = side_by_side(
+                one, first, two, second, masks_ref
             )
+        for n, group in enumerate(GROUPS):
+            shared = None
+            for t in group:
+                way = lane + DIRECTIONS.index(t)
+                tile, half = tile_of(index_ref, index_row, way, table_ref, part)
+                piece = masked(tile, masks_ref[3 + 2 * kind_of(t) + half])
+                shared = piece if shared is None else shared + piece
+            gathered_ref[rows, n * 128 : (n + 1) * 128] = shared
         return carry
 
-    lax.fori_loop(0, bricks, brick, 0)
+    if bricks > 1:
+        lax.fori_loop(0, bricks, brick, 0)
+    else:
+        brick(0, 0)
     out_ref[:, 384:512] = mm(gathered_ref[...], choose).astype(BF16)
 
 
-def pack_octants(bricks, channels, index_ref, dest, base, table_ref, out_ref, gathered_ref, choose):
-    low = lax.broadcasted_iota(I32, (channels, 128), 1) < 64
+def pack_octants(bricks, part, index_ref, dest, base, table_ref, out_ref, gathered_ref, choose, masks_ref):
+    channels = part.size
     for b in range(bricks):
         rows = slice(b * channels, (b + 1) * channels)
         line = base + b
         index_row, lane = dest * LINK_ROWS + line // LINK_ROWS, line % LINK_ROWS * 32
         for way in range(0, 8, 2):
-            one, first = tile_of(index_ref, index_row, lane + way, table_ref)
-            two, second = tile_of(index_ref, index_row, lane + way + 1, table_ref)
-            one = either_half(first, one, low, 0)
-            two = either_half(second, two, low, 1)
-            gathered_ref[rows, way * 64 : way * 64 + 128] = jnp.where(low, one, two)
+            one, first = tile_of(index_ref, index_row, lane + way, table_ref, part)
+            two, second = tile_of(index_ref, index_row, lane + way + 1, table_ref, part)
+            gathered_ref[rows, way * 64 : way * 64 + 128] = side_by_side(
+                one, first, two, second, masks_ref
+            )
     out_ref[...] = mm(gathered_ref[...], choose).astype(BF16)
 
 
@@ -370,13 +436,16 @@
     come_ref,
     gathered_ref,
     choose_ref,
+    masks_ref,
     send_sems,
     recv_sems,
+    chunks,
     tables=None,
     meanwhile=None,
 ):
     y, core, x, z = place_self()
-    half = channels // 2
+    width = channels // chunks
+    half = width // 2
 
     def at(dy, dx, dz, new_core):
         return (((y + dy) % RING) * CORES + new_core, ((x + dx) % RING) * RING + (z + dz) % RING)
@@ -384,10 +453,10 @@
     def peer(dy, dz):
         return at(dy, 0, dz, core)
 
-    def block(dy, dz, other=False):
+    def block(dy, dz, other=False, first_row=0, count=rows):
         new_core = 1 - core if other else core
         member = (((y + dy) % RING) * CORES + new_core) * RING + (z + dz) % RING
-        return pl.ds(member * rows, rows)
+        return pl.ds(member * rows + first_row, count)
 
     other_core = at(0, 0, 0, 1 - core)
     along_x = [at(0, k, 0, core) for k in (1, 2, 3)]
@@ -427,40 +496,159 @@
             device_id_type=MESH,
         ).wait_recv()
 
-    def send(dy, dz, start, size, device):
-        part = pl.ds(start, size)
-        source = own_ref.at[:, part] if (dy, dz) == (0, 0) else all_ref.at[block(dy, dz), part]
-        return remote(source, all_ref.at[block(dy, dz), part], device)
-
-    siblings = []
-
-    def sibling(dy, dz, start, size):
-        siblings.append((send(dy, dz, start, size, other_core), dy, dz, start, size))
+    def view(dy, dz, region, other=False):
+        row, count, start, size = region
+        return all_ref.at[block(dy, dz, other, row, count), pl.ds(start, size)]
+
+    def send(dy, dz, region, device):
+        row, count, start, size = region
+        source = view(dy, dz, region)
+        if (dy, dz) == (0, 0):
+            source = own_ref.at[pl.ds(row, count), pl.ds(start, size)]
+        return remote(source, view(dy, dz, region), device)
 
     UP, DOWN = 1, 3
 
     def off(axis, k):
         return (k % RING, 0) if axis == "y" else (0, k % RING)
 
-    def both(axis, dy, dz, start, size):
+    def both(axis, dy, dz, region):
         events = []
         for step in (UP, DOWN):
             sy, sz = off(axis, step)
-            n = send(dy, dz, start, size, peer(sy, sz))
-            events.append((n, axis, step, (dy - sy) % RING, (dz - sz) % RING, start, size))
+            n = send(dy, dz, region, peer(sy, sz))
+            events.append((n, axis, step, (dy - sy) % RING, (dz - sz) % RING, region))
         return events
 
     def relay(event):
-        n, axis, step, dy, dz, start, size = event
-        piece = size // 2
-        begin = start if step == UP else start + piece
+        n, axis, step, dy, dz, (row, count, start, size) = event
+        if size // 2 >= 16:
+            begin = start if step == UP else start + size // 2
+            region = (row, count, begin, size // 2)
+        else:
+            region = (row if step == UP else row + count // 2, count // 2, start, size)
         sy, sz = off(axis, step)
-        m = send(dy, dz, begin, piece, peer(sy, sz))
-        return (m, axis, step, (dy - sy) % RING, (dz - sz) % RING, begin, piece)
+        m = send(dy, dz, region, peer(sy, sz))
+        return (m, axis, step, (dy - sy) % RING, (dz - sz) % RING, region)
 
     def wait(event):
-        n, _, _, dy, dz, start, size = event
-        landed(n, all_ref.at[block(dy, dz), pl.ds(start, size)])
+        n, _, _, dy, dz, region = event
+        landed(n, view(dy, dz, region))
+
+    class Gather:
+        def __init__(self, chunk):
+            start = chunk * width
+            self.whole = (0, rows, start, width)
+            self.axes = [("z", "y", (0, rows, start, half)), ("y", "z", (0, rows, start + half, half))]
+            self.second, self.siblings, self.last = [], [], []
+
+        def sibling(self, dy, dz, region):
+            self.siblings.append((send(dy, dz, region, other_core), dy, dz, region))
+
+        def begin(self):
+            self.ahead = [both(axis, 0, 0, region) for axis, _, region in self.axes]
+            for _, axis, region in self.axes:
+                self.second += both(axis, 0, 0, region)
+            self.sibling(0, 0, self.whole)
+
+        def neighbours(self):
+            relays = []
+            for (_, axis, region), events in zip(self.axes, self.ahead):
+                passed = []
+                for event in events:
+                    wait(event)
+                    passed.append(relay(event))
+                    self.second += both(axis, event[3], event[4], region)
+                    self.sibling(event[3], event[4], region)
+                relays.append(passed)
+            for (_, axis, region), passed in zip(self.axes, relays):
+                for event in passed:
+                    wait(event)
+                dy, dz = passed[0][3:5]
+                self.second += both(axis, dy, dz, region)
+                self.sibling(dy, dz, region)
+
+        def forward(self, count):
+            for event in self.second[:count]:
+                wait(event)
+                self.last.append(relay(event))
+                self.sibling(*event[3:])
+            self.second = self.second[count:]
+
+        def finish(self):
+            self.forward(len(self.second))
+            for event in self.last:
+                wait(event)
+                self.sibling(*event[3:])
+            for n, dy, dz, region in self.siblings:
+                landed(n, view(dy, dz, region, True))
+
+    size = bricks * width
+    low, high = pl.ds(0, size // 2), pl.ds(size // 2, size // 2)
+    packer = pack_halo if halo else pack_octants
+    up, down = along_x[0], along_x[2]
+
+    class Exchange:
+        def __init__(self, chunk):
+            self.chunk = chunk
+
+        def at(self, ref, *place):
+            return ref.at[(*place[:-1], self.chunk, place[-1])]
+
+        def pack(self, k):
+            packer(
+                bricks,
+                pl.ds(self.chunk * width, width),
+                index_ref,
+                (x + k) % RING,
+                base,
+                all_ref,
+                parts_ref.at[k, self.chunk],
+                gathered_ref,
+                choose_ref[...],
+                masks_ref,
+            )
+
+        def far(self):
+            self.pack(2)
+            self.far_up = remote(self.at(parts_ref, 2, low), self.at(stage_ref, low), up)
+            self.far_down = remote(self.at(parts_ref, 2, high), self.at(stage_ref, high), down)
+
+        def near_up(self):
+            self.pack(1)
+            self.ups = [remote(self.at(parts_ref, 1, high), self.at(come_ref, 0, high), up)]
+
+        def near_down(self):
+            self.pack(3)
+            self.downs = [remote(self.at(parts_ref, 3, low), self.at(come_ref, 1, low), down)]
+
+        def add(self, k, rows):
+            place = (k, self.chunk, rows)
+            more = stage_ref[self.chunk, rows].astype(F32)
+            parts_ref[place] = (parts_ref[place].astype(F32) + more).astype(BF16)
+
+        def passed_on(self):
+            landed(self.far_up, self.at(stage_ref, low))
+            self.add(1, low)
+            self.ups.append(remote(self.at(parts_ref, 1, low), self.at(come_ref, 0, low), up))
+            landed(self.far_down, self.at(stage_ref, high))
+            self.add(3, high)
+            self.downs.append(remote(self.at(parts_ref, 3, high), self.at(come_ref, 1, high), down))
+
+        def finish(self):
+            landed(self.ups[0], self.at(come_ref, 0, high))
+            landed(self.downs[0], self.at(come_ref, 1, low))
+            landed(self.ups[1], self.at(come_ref, 0, low))
+            landed(self.downs[1], self.at(come_ref, 1, high))
+            for b in range(bricks):
+                part = pl.ds(b * width, width)
+                total = (
+                    parts_ref[0, self.chunk, part].astype(F32)
+                    + come_ref[0, self.chunk, part].astype(F32)
+                    + come_ref[1, self.chunk, part].astype(F32)
+                )
+                begin = b * channels + self.chunk * width
+                out_ref[begin : begin + width] = total.astype(BF16)
 
     arrivals = []
     if tables:
@@ -476,124 +664,93 @@
         all_sends[own_member] = owed_ref[y * CORES + core]
         all_links[x] = asked_ref[...]
 
-    axes = [("z", "y", 0), ("y", "z", half)]
-    ahead = [both(axis, 0, 0, start, half) for axis, _, start in axes]
-    second = []
-    for _, axis, start in axes:
-        second += both(axis, 0, 0, start, half)
-    sibling(0, 0, 0, channels)
-
-    relays = []
-    for (_, axis, start), events in zip(axes, ahead):
-        passed = []
-        for event in events:
-            wait(event)
-            passed.append(relay(event))
-            second += both(axis, event[3], event[4], start, half)
-            sibling(event[3], event[4], start, half)
-        relays.append(passed)
-    for (_, axis, start), passed in zip(axes, relays):
-        for event in passed:
-            wait(event)
-        dy, dz = passed[0][3:5]
-        second += both(axis, dy, dz, start, half)
-        sibling(dy, dz, start, half)
-
-    def settle():
-        last = []
-        for event in second:
-            wait(event)
-            last.append(relay(event))
-            sibling(*event[3:])
-        for event in last:
-            wait(event)
-            sibling(*event[3:])
-        for n, dy, dz, start, size in siblings:
-            landed(n, all_ref.at[block(dy, dz, True), pl.ds(start, size)])
-
-    for n, view in arrivals:
-        landed(n, view)
+    gathers = [Gather(chunk) for chunk in range(chunks)]
+    exchanges = [Exchange(chunk) for chunk in range(chunks)]
+    gathers[0].begin()
+    gathers[0].neighbours()
+    if chunks > 1:
+        gathers[1].begin()
+    for n, arrival in arrivals:
+        landed(n, arrival)
     if meanwhile:
         meanwhile()
-    settle()
-    packer = pack_halo if halo else pack_octants
-
-    size = bricks * channels
-    low, high = pl.ds(0, size // 2), pl.ds(size // 2, size // 2)
-
-    def pack(k):
-        packer(
-            bricks,
-            channels,
-            index_ref,
-            (x + k) % RING,
-            base,
-            all_ref,
-            parts_ref.at[k],
-            gathered_ref,
-            choose_ref[...],
-        )
-
-    up, down = along_x[0], along_x[2]
-    pack(2)
-    far_up = remote(parts_ref.at[2, low], stage_ref.at[low], up)
-    far_down = remote(parts_ref.at[2, high], stage_ref.at[high], down)
-    pack(1)
-    near_up = [remote(parts_ref.at[1, high], come_ref.at[0, high], up)]
-    pack(3)
-    near_down = [remote(parts_ref.at[3, low], come_ref.at[1, low], down)]
-    landed(far_up, stage_ref.at[low])
-    parts_ref[1, low] = (parts_ref[1, low].astype(F32) + stage_ref[low].astype(F32)).astype(BF16)
-    landed(far_down, stage_ref.at[high])
-    parts_ref[3, high] = (parts_ref[3, high].astype(F32) + stage_ref[high].astype(F32)).astype(BF16)
-    near_up.append(remote(parts_ref.at[1, low], come_ref.at[0, low], up))
-    near_down.append(remote(parts_ref.at[3, high], come_ref.at[1, high], down))
-    pack(0)
-    landed(near_up[0], come_ref.at[0, high])
-    landed(near_down[0], come_ref.at[1, low])
-    landed(near_up[1], come_ref.at[0, low])
-    landed(near_down[1], come_ref.at[1, high])
-    total = parts_ref[0].astype(F32) + come_ref[0].astype(F32) + come_ref[1].astype(F32)
-    out_ref[...] = total.astype(BF16)
+    gathers[0].forward(len(gathers[0].second))
+    if chunks > 1:
+        gathers[1].neighbours()
+    gathers[0].finish()
+
+    def tick(count):
+        if chunks > 1:
+            gathers[1].forward(count)
+
+    exchanges[0].far()
+    tick(4)
+    exchanges[0].near_up()
+    tick(4)
+    exchanges[0].near_down()
+    tick(4)
+    exchanges[0].passed_on()
+    tick(4)
+    exchanges[0].pack(0)
+    if chunks > 1:
+        gathers[1].finish()
+        exchanges[1].far()
+        exchanges[1].near_up()
+        exchanges[1].near_down()
+        exchanges[1].passed_on()
+        exchanges[1].pack(0)
+    for exchange in exchanges:
+        exchange.finish()
     for copy in started:
         copy.wait_send()
 
 
-COPIES = 79 + 34 + 6
+COPIES = 2 * (79 + 6) + 34
 
 
 def body_kernel(bricks, channels, *refs):
     (
-        voxels, gain0, gain1, gain2, lift1, lift2, constants, faces, corners, octants, places, shifts
-    ) = refs[:12]
-    sends, links = refs[12:17], refs[17:22]
-    kernel0_hbm, kernel1_hbm = refs[22:24]
-    out0_hbm, out1_hbm, hidden2, active2, halo2 = refs[24:29]
+        voxels, gain0, gain1, gain2, lift1, lift2, constants, faces, corners, octants, places, shifts,
+        kinds,
+    ) = refs[:13]
+    sends, links = refs[13:18], refs[18:23]
+    kernel0_hbm, kernel1_hbm, kernel2_hbm = refs[23:26]
+    out0_hbm, out1_hbm, out2 = refs[26:29]
     (
         owed, asked, all_sends, all_links, found, index,
         active0, hidden1, active1, out0, out1, halo0, halo1, grid1, grid2,
         own0, own1, own2, pooled0, pooled1,
-        kernel0, kernel1, weight0, weight1,
+        kernel0, weight0, weight1, weight2, hidden2, active2, halo2,
         choose_corners, choose_octants, place_matrix, shift_matrix,
         gathered, source, padded, moved,
-    ) = refs[29:61]
-    buffers = [refs[61 + 4 * n : 65 + 4 * n] for n in range(5)]
-    send_sems, recv_sems, local_sems = refs[81:]
+    ) = refs[29:64]
+    buffers = [refs[64 + 4 * n : 68 + 4 * n] for n in range(5)]
+    masks, send_sems, recv_sems, local_sems, weight_sems = refs[84:]
 
     count = greet()
-    fetch = [
-        pltpu.make_async_copy(kernel0_hbm, kernel0, local_sems.at[0]),
-        pltpu.make_async_copy(kernel1_hbm, kernel1, local_sems.at[1]),
-    ]
-    for copy in fetch:
-        copy.start()
+    fetch = pltpu.make_async_copy(kernel0_hbm, kernel0, local_sems.at[0])
+    fetch.start()
+
+    def blocks(level, kernel_hbm, weight):
+        side = channels[level]
+        return [
+            pltpu.make_async_copy(
+                kernel_hbm.at[n],
+                weight.at[pl.ds(n // 9 * side, side), pl.ds(n % 9 * side, side)],
+                weight_sems.at[level - 1, n],
+            )
+            for n in range(27)
+        ]
+
+    weights = blocks(1, kernel1_hbm, weight1) + blocks(2, kernel2_hbm, weight2)
     list_slots(sends, links, owed, asked)
+    write_masks(masks, kinds)
     enter_fine(bricks[0], channels[0], voxels, gain0, faces, active0, own0)
     pl.semaphore_wait(pltpu.get_barrier_semaphore(), count)
 
     def meanwhile():
         resolve(found, all_links, all_sends, constants)
-        depth = len(CORNERS) * 128
+        depth = len(GROUPS) * 128
         at_row = lax.broadcasted_iota(I32, (depth, 128), 0)
         at_row = lax.shift_left(lax.shift_right_logical(at_row, 7), 6) + (at_row & 63)
         choose_corners[...] = jnp.where(at_row == corners[...], 1.0, 0.0).astype(BF16)
@@ -602,14 +759,15 @@
         choose_octants[...] = selection(512, octants[...])
         shift_matrix[...] = selection(256, shifts[...])
         tell.wait()
-        for copy in fetch:
-            copy.wait()
+        fetch.wait()
         arrange(channels[0], kernel0, weight0)
+        for copy in weights:
+            copy.start()
 
     def step(n, level, halo, base, own, out, **more):
         below = channels[level] if halo else channels[level - 1]
         size = bricks[level] * below
-        wide = len(CORNERS) * 128 if halo else 512
+        wide = len(GROUPS) * 128 if halo else 512
         trade(
             bricks[level],
             below,
@@ -620,10 +778,12 @@
             index,
             out,
             *buffers[n],
-            gathered.at[pl.ds(0, size), pl.ds(0, wide)],
+            gathered.at[pl.ds(0, size // CHUNKS[n]), pl.ds(0, wide)],
             choose_corners if halo else choose_octants,
-            send_sems.at[n % 2],
+            masks,
+            send_sems,
             recv_sems.at[n % 2],
+            CHUNKS[n],
             **more,
         )
 
@@ -653,7 +813,9 @@
     keep0 = pltpu.make_async_copy(out0, out0_hbm, local_sems.at[3])
     keep0.start()
     pool(bricks[0], channels[0], out0, pooled0)
-    step(1, 1, False, lines[3], pooled0, grid1, meanwhile=lambda: arrange(channels[1], kernel1, weight1))
+    step(1, 1, False, lines[3], pooled0, grid1)
+    for copy in weights:
+        copy.wait()
     enter_coarser(
         bricks[1], channels[0], channels[1], True, grid1, lift1, gain1, faces, hidden1, active1, own1
     )
@@ -667,50 +829,14 @@
         bricks[2], channels[1], channels[2], False, grid2, lift2, gain2, faces, hidden2, active2, own2
     )
     step(4, 2, True, lines[2], own2, halo2)
+    leave(2, active2, halo2, hidden2, weight2, out2)
     keep0.wait()
     keep1.wait()
 
 
-def last_kernel(
-    bricks,
-    channels,
-    active_ref,
-    halo_ref,
-    hidden_ref,
-    kernel_ref,
-    places_ref,
-    shifts_ref,
-    fine_ref,
-    middle_ref,
-    fine_out,
-    middle_out,
-    out_ref,
-    place_matrix,
-    shift_matrix,
-    weight_ref,
-    source_ref,
-    padded_ref,
-    moved_ref,
-):
-    fine_out[...] = fine_ref[...]
-    middle_out[...] = middle_ref[...]
-    place_matrix[...] = selection(1024, places_ref[...])
-    shift_matrix[...] = selection(256, shifts_ref[...])
-    arrange(channels, kernel_ref, weight_ref)
-    convolve(
-        bricks,
-        channels,
-        active_ref,
-        halo_ref,
-        hidden_ref,
-        weight_ref,
-        place_matrix,
-        shift_matrix,
-        out_ref,
-        source_ref,
-        padded_ref,
-        moved_ref,
-    )
+def hand_on(*refs):
+    for n in range(3):
+        refs[3 + n][...] = refs[n][...]
 
 
 def per_device(
@@ -778,39 +904,45 @@
         vmem(*pooled[0]),
         vmem(*pooled[1]),
         vmem(*kernel_fine.shape),
-        vmem(*kernel_middle.shape),
         vmem(3 * channels[0], 9 * channels[0]),
         vmem(3 * channels[1], 9 * channels[1]),
-        vmem(len(CORNERS) * 128, 128),
+        vmem(3 * channels[2], 9 * channels[2]),
+        vmem(sizes[2], 512),
+        vmem(sizes[2], 512),
+        vmem(sizes[2], 512),
+        vmem(len(GROUPS) * 128, 128),
         vmem(512, 512),
         vmem(1024, 1280),
         vmem(256, 1152),
-        vmem(max(sizes), len(CORNERS) * 128),
+        vmem(max(sizes) // (1 if CHUNKS[0] == 1 else 2), len(GROUPS) * 128),
         vmem(max(sizes[:2]), 1024),
         vmem(max(sizes[:2]), 1280),
-        vmem(9 * channels[1], 640),
+        vmem(9 * channels[2], 640),
     ]
-    for table, size in zip(
+    for table, size, chunks in zip(
         (owns[0], pooled[0], owns[1], pooled[1], owns[2]),
         (sizes[0], grids[0], sizes[1], grids[1], sizes[2]),
+        CHUNKS,
     ):
         scratch += [
             vmem(MEMBERS * table[0] + 1, table[1], 128),
-            vmem(RING, size, 512),
-            vmem(size, 512),
-            vmem(2, size, 512),
+            vmem(RING, chunks, size // chunks, 512),
+            vmem(chunks, size // chunks, 512),
+            vmem(2, chunks, size // chunks, 512),
         ]
     scratch += [
-        pltpu.SemaphoreType.DMA((2, COPIES)),
+        vmem(3 + 2 * len(KINDS), 16, 128),
+        pltpu.SemaphoreType.DMA((COPIES,)),
         pltpu.SemaphoreType.DMA((2, COPIES)),
         pltpu.SemaphoreType.DMA((5,)),
+        pltpu.SemaphoreType.DMA((2, 27)),
     ]
     anywhere = pl.BlockSpec(memory_space=pl.ANY)
-    fine, middle, hidden, active, halo = pl.pallas_call(
+    results = pl.pallas_call(
         functools.partial(body_kernel, bricks, channels),
-        out_shape=[shape(sizes[0], 512), shape(sizes[1], 512)] + [shape(sizes[2], 512)] * 3,
-        in_specs=whole(22) + [anywhere] * 2,
-        out_specs=[anywhere] * 2 + whole(3),
+        out_shape=[shape(size, 512) for size in sizes],
+        in_specs=whole(23) + [anywhere] * 3,
+        out_specs=[anywhere] * 2 + whole(1),
         scratch_shapes=scratch,
         compiler_params=pltpu.CompilerParams(
             collective_id=0, has_side_effects=True, vmem_limit_bytes=VMEM_LIMIT
@@ -827,27 +959,19 @@
         jnp.asarray(octant_sources()),
         places,
         shifts,
+        jnp.asarray(kind_masks()),
         *sends,
         *links,
-        kernel_fine,
-        kernel_middle,
+        *kernels,
     )
     outputs = pl.pallas_call(
-        functools.partial(last_kernel, bricks[2], channels[2]),
+        hand_on,
         out_shape=[shape(size, 512) for size in sizes],
-        in_specs=whole(8),
+        in_specs=whole(3),
         out_specs=whole(3),
-        scratch_shapes=[
-            vmem(1024, 1280),
-            vmem(256, 1152),
-            vmem(3 * channels[2], 9 * channels[2]),
-            vmem(sizes[2], 1024),
-            vmem(sizes[2], 1280),
-            vmem(9 * channels[2], 640),
-        ],
         compiler_params=PARAMS,
-        name="last",
-    )(active, halo, hidden, kernel_coarse, places, shifts, fine, middle)
+        name="hand_on",
+    )(*results)
     return tuple(
         out.reshape(b, c, 512) for out, b, c in zip(outputs, bricks, channels)
     )

time: 213 us -> 212 us (level)
    pallas_call x1, Pallas kernels: 8.13 us -> 2.17 us  [per_device(): pl.pallas_call(hand_on, out_shape=[shape(size, 512) for size in sizes], i...]
    pallas_call x1, Pallas kernels: 204 us -> 209 us  [per_device(): pl.pallas_call(functools.partial(body_kernel, bricks, channels), out_shap...]
where the time goes in v4:
time: 212 us
  Pallas kernels  211 us (100%)
    pallas_call x1, Pallas kernels, per_device(): pl.pallas_call(functools.partial(body_kernel, bricks, channels), out_shap...  209 us

profile of v4, /device:TPU:1, one launch (start us, length us, event | category | flops | bytes accessed | tf_op | source)
XLA Modules:
  0.0 211.6 jit_solution(16507109508958907917)
XLA Ops:
  0.6 208.8 %levels.1 = (bf16[512,512]{1,0:T(8,128)(2,1)}, bf16[256,512]{1,0:T(8,128)(2,1)}, bf16[256,512]{1,0:T(8,128)(2,1)}) custom-call(bf16[512,512]{1,0:T(8,128)(2,1)} %bitcast.8, f32[1,64]{1,0:T(1,128)} %bitcast.11, f32[1,128]{1,0:T(1,128)} %bitcast.12, f32[1,256]{1,0:T(1,128)} %bitcast.10, bf16[64,128]{1,0:T(8,128)(2,1)} %bitcast.9, bf16[256,128]{1,0:T(8,128)(2,1)} %refs_5_.1, ...), custom_call_target="tpu_custom_call" | custom-call | tf_op jit(solution)/shard_map/levels/pallas_call | solution.py:941
  209.4 2.2 %hand_on.1 = (bf16[512,512]{1,0:T(8,128)(2,1)}, bf16[256,512]{1,0:T(8,128)(2,1)}, bf16[256,512]{1,0:T(8,128)(2,1)}) custom-call(bf16[512,512]{1,0:T(8,128)(2,1)} %get-tuple-element.9.refs_0_, bf16[256,512]{1,0:T(8,128)(2,1)} %get-tuple-element.10.refs_1_, bf16[256,512]{1,0:T(8,128)(2,1)} %get-tuple-element.11.refs_2_), custom_call_target="tpu_custom_call" | custom-call | tf_op jit(solution)/shard_map/hand_on/pallas_call | solution.py:967
